TPU v7x, 32 devices: a whole 2x2x4 slice. The times are simulated.
32 devices in a mesh: ep: 8 (over z, x), tp: 4 (over y, core).
Axes of the slice: x: 2, y: 2, z: 4, core: 2. Of those that a mesh axis runs over, the one named last changes fastest.
Arguments:
- tokens: bfloat16 [1024, 3072], P('ep', 'tp'), may hold values from -6 to 6
- expert_ids: int32 [1024, 2], P('ep'), may hold values from 0 to 7, all different within a row
- route_share: float32 [1024], P('ep'), may hold values from 0.5 to 0.95
- w_gate: bfloat16 [65536, 3072], P(('ep', 'tp')), may hold values from -0.109375 to 0.109375
- w_up: bfloat16 [65536, 3072], P(('ep', 'tp')), may hold values from -0.109375 to 0.109375
- w_down: bfloat16 [65536, 3072], P(('ep', 'tp')), may hold values from -0.0625 to 0.0625
- reward_head: float32 [3072], P('tp'), may hold values from -0.109375 to 0.109375
- upstream: bfloat16 [1024, 3072], P('ep', 'tp'), may hold values from -4 to 4
- pair_order: int32 [16], replicated, may hold values from 0 to 15, each once
Outputs:
- layer_out: bfloat16 [1024, 3072], P('ep', 'tp')
- rewards: float32 [16], replicated
- pair_loss: float32 [], replicated
- grad_tokens: bfloat16 [1024, 3072], P('ep', 'tp')
- grad_gate: bfloat16 [65536, 3072], P(('ep', 'tp'))
- grad_up: bfloat16 [65536, 3072], P(('ep', 'tp'))
- grad_down: bfloat16 [65536, 3072], P(('ep', 'tp'))
Inputs may be any that keep to these rules, and one draw needn't show every extreme that they name: `expert_ids`: each row names 2 different experts. `pair_order`: each of the 16 sequence indices appears once.
All inputs are finite; a program needn't handle non-finite values.
Results may differ from a plain program's by a relative error of at most 0.014.
Values may be sent and summed in bfloat16 or wider, within the bound.
A program may use at most 128 MiB of HBM per device.

v0:
```python
import math
from functools import partial

import jax
import jax.numpy as jnp
from jax import lax
from jax.experimental import pallas as pl
from jax.experimental.pallas import tpu as pltpu
from jax.sharding import PartitionSpec as P

EXPERTS = 8
SEQ_LEN = 64


loss_scale = 256.0
highest = lax.Precision.HIGHEST


def route_tables(expert_ids, route_share, capacity):
    experts_iota = jnp.arange(EXPERTS, dtype=jnp.int32)
    first_hot = (expert_ids[:, 0:1] == experts_iota[None, :]).astype(jnp.int32)
    second_hot = (expert_ids[:, 1:2] == experts_iota[None, :]).astype(jnp.int32)
    first_rank = jnp.sum((jnp.cumsum(first_hot, axis=0) - first_hot) * first_hot, axis=1)
    second_before = (
        jnp.cumsum(second_hot, axis=0) - second_hot + jnp.sum(first_hot, axis=0)[None, :]
    )
    second_rank = jnp.sum(second_before * second_hot, axis=1)
    route_ranks = jnp.stack([first_rank, second_rank], axis=1)
    route_kept = route_ranks < capacity
    slot_index = jnp.where(route_kept, expert_ids * capacity + route_ranks, -1)
    shares = jnp.stack([route_share, 1.0 - route_share], axis=1) * route_kept.astype(jnp.float32)
    slot_iota = jnp.arange(EXPERTS * capacity, dtype=jnp.int32)
    matches = (slot_index[:, :, None] == slot_iota[None, None, :]).astype(jnp.float32)
    picker = jnp.sum(matches, axis=1)
    mixing = jnp.sum(matches * shares[:, :, None], axis=1)
    return (picker, mixing)


def silu_parts(gate_pre):
    sigmoid_value = jax.nn.sigmoid(gate_pre)
    return (gate_pre * sigmoid_value, sigmoid_value * (1.0 + gate_pre * (1.0 - sigmoid_value)))


def slot_buffer(picker, source_rows, capacity):
    selected = lax.dot_general(
        picker.astype(jnp.bfloat16),
        source_rows,
        (((0,), (0,)), ((), ())),
        preferred_element_type=jnp.float32,
    )
    return selected.astype(jnp.bfloat16).reshape(EXPERTS, capacity, source_rows.shape[1])


MESH = pl.DeviceIdType.MESH


def remote(src, dst, send_sem, recv_sem, target):
    return pltpu.make_async_remote_copy(
        src_ref=src,
        dst_ref=dst,
        send_sem=send_sem,
        recv_sem=recv_sem,
        device_id=target,
        device_id_type=MESH,
    )


def spread_kernel(
    n_ep, n_tp, tok_ref, ups_ref, meta_ref, head_ref, tok_out, ups_out, meta_out, head_out,
    local_sem, tok_send, ups_send, meta_send, head_send, tp_send,
    tok_recv, ups_recv, meta_recv, head_recv, tp_recv,
):
    q = lax.axis_index("ep")
    t = lax.axis_index("tp")
    width = tok_ref.shape[2]
    replicas = n_ep // tok_ref.shape[0]
    partner = t + 1 - 2 * (t % 2)

    barrier = pltpu.get_barrier_semaphore()
    for k in range(1, n_ep):
        pl.semaphore_signal(barrier, inc=1, device_id=((q + k) % n_ep, t), device_id_type=MESH)
    for k in range(1, n_tp):
        pl.semaphore_signal(barrier, inc=1, device_id=(q, (t + k) % n_tp), device_id_type=MESH)
    pl.semaphore_wait(barrier, n_ep + n_tp - 2)

    def columns(owner):
        return pl.ds(pl.multiple_of(owner * width, 128), width)

    own = q // replicas
    local = [
        pltpu.make_async_copy(tok_ref.at[own], tok_out.at[q, :, columns(t)], local_sem.at[0]),
        pltpu.make_async_copy(ups_ref.at[own], ups_out.at[q], local_sem.at[1]),
        pltpu.make_async_copy(meta_ref.at[own], meta_out.at[q], local_sem.at[2]),
        pltpu.make_async_copy(head_ref, head_out.at[t], local_sem.at[3]),
    ]
    for copy in local:
        copy.start()
    for k in range(1, n_ep):
        to = (q + k) % n_ep
        remote(
            tok_ref.at[to // replicas], tok_out.at[q, :, columns(t)],
            tok_send, tok_recv.at[k], (to, t),
        ).start()
    for k in range(1, n_tp):
        remote(
            head_ref, head_out.at[t], head_send, head_recv.at[k], (q, (t + k) % n_tp)
        ).start()
    for k in range(1, n_ep):
        to = (q + k) % n_ep
        remote(
            meta_ref.at[to // replicas], meta_out.at[q], meta_send, meta_recv.at[k], (to, t)
        ).start()
        remote(
            ups_ref.at[to // replicas], ups_out.at[q], ups_send, ups_recv.at[k], (to, t)
        ).start()

    def hand_on(k, owner, target, row):
        piece = tok_out.at[(q + n_ep - k) % n_ep, :, columns(owner)]
        return remote(piece, piece, tp_send, tp_recv.at[row, k], (q, target))

    def forward(k):
        for j in range(1, n_tp // 2):
            origin = (t + n_tp - 2 * j) % n_tp
            hand_on(k, origin, t, j - 1).wait_recv()
            hand_on(k, origin, partner, n_tp // 2 - 1 + j).start()

    lag = 2
    for k in range(n_ep):
        if k == 0:
            local[0].wait()
        else:
            source = (q + n_ep - k) % n_ep
            remote(
                tok_ref.at[0], tok_out.at[source, :, columns(t)],
                tok_send, tok_recv.at[k], (source, t),
            ).wait_recv()
        for j in range(1, n_tp // 2):
            hand_on(k, t, (t + 2 * j) % n_tp, j - 1).start()
        hand_on(k, t, partner, n_tp // 2 - 1).start()
        if k >= lag:
            forward(k - lag)
    for k in range(max(n_ep - lag, 0), n_ep):
        forward(k)
    for k in range(n_ep):
        hand_on(k, partner, t, n_tp // 2 - 1).wait_recv()
        for j in range(1, n_tp // 2):
            origin = (partner + n_tp - 2 * j) % n_tp
            hand_on(k, origin, t, n_tp // 2 - 1 + j).wait_recv()
    for copy in local[1:]:
        copy.wait()
    for k in range(1, n_tp):
        source = (t + n_tp - k) % n_tp
        remote(head_ref, head_out.at[source], head_send, head_recv.at[k], (q, source)).wait_recv()
    for k in range(1, n_ep):
        source = (q + n_ep - k) % n_ep
        remote(
            meta_ref.at[0], meta_out.at[source], meta_send, meta_recv.at[k], (source, t)
        ).wait_recv()
        remote(
            ups_ref.at[0], ups_out.at[source], ups_send, ups_recv.at[k], (source, t)
        ).wait_recv()

    def drain(sent, sem):
        pltpu.make_async_copy(sent, sent, sem).wait()

    drain(ups_out.at[pl.ds(0, n_ep - 1)], tok_send)
    drain(ups_out.at[pl.ds(0, n_ep - 1)], ups_send)
    drain(meta_out.at[pl.ds(0, n_ep - 1)], meta_send)
    drain(head_out.at[pl.ds(0, n_tp - 1)], head_send)
    drain(tok_out.at[:, :, pl.ds(0, (n_tp - 1) * width)], tp_send)


def spread_slots(tok_buf, ups_buf, meta, head_rows):
    n_ep = lax.axis_size("ep")
    n_tp = lax.axis_size("tp")
    experts, capacity, width = tok_buf.shape
    dma = pltpu.SemaphoreType.DMA
    vmem = pl.BlockSpec(memory_space=pltpu.VMEM)
    return pl.pallas_call(
        partial(spread_kernel, n_ep, n_tp),
        out_shape=(
            jax.ShapeDtypeStruct((n_ep, capacity, n_tp * width), jnp.bfloat16),
            jax.ShapeDtypeStruct((n_ep, capacity, width), jnp.bfloat16),
            jax.ShapeDtypeStruct((n_ep,) + meta.shape[1:], jnp.float32),
            jax.ShapeDtypeStruct((n_tp,) + head_rows.shape, jnp.float32),
        ),
        in_specs=[vmem] * 4,
        out_specs=[vmem] * 4,
        scratch_shapes=[
            dma((4,)), dma, dma, dma, dma, dma,
            dma((n_ep,)), dma((n_ep,)), dma((n_ep,)), dma((n_tp,)), dma((n_tp - 1, n_ep)),
        ],
        compiler_params=pltpu.CompilerParams(collective_id=0, has_side_effects=True),
        name="spread_slots",
    )(tok_buf, ups_buf, meta, head_rows)


def share_kernel(n_ep, n_tp, mine_ref, all_ref, local_sem, send_sem, recv_sem):
    q = lax.axis_index("ep")
    t = lax.axis_index("tp")
    count = n_ep * n_tp
    me = q * n_tp + t
    barrier = pltpu.get_barrier_semaphore()

    def greet(k, carry):
        other = (me + k) % count
        pl.semaphore_signal(
            barrier, inc=1, device_id=(other // n_tp, other % n_tp), device_id_type=MESH
        )
        return carry

    lax.fori_loop(1, count, greet, 0)
    pl.semaphore_wait(barrier, count - 1)
    own = pltpu.make_async_copy(mine_ref, all_ref.at[me], local_sem)
    own.start()

    def send(k, carry):
        other = (me + k) % count
        remote(
            mine_ref, all_ref.at[me], send_sem, recv_sem, (other // n_tp, other % n_tp)
        ).start()
        return carry

    lax.fori_loop(1, count, send, 0)
    own.wait()
    rest = all_ref.at[pl.ds(0, count - 1)]
    pltpu.make_async_copy(rest, rest, recv_sem).wait()
    pltpu.make_async_copy(rest, rest, send_sem).wait()


def share_rows(mine):
    n_ep = lax.axis_size("ep")
    n_tp = lax.axis_size("tp")
    dma = pltpu.SemaphoreType.DMA
    vmem = pl.BlockSpec(memory_space=pltpu.VMEM)
    return pl.pallas_call(
        partial(share_kernel, n_ep, n_tp),
        out_shape=jax.ShapeDtypeStruct((n_ep * n_tp,) + mine.shape, jnp.float32),
        in_specs=[vmem],
        out_specs=vmem,
        scratch_shapes=[dma, dma, dma],
        compiler_params=pltpu.CompilerParams(collective_id=1, has_side_effects=True),
        name="share_rows",
    )(mine)


def return_sums(sums, local_width, replicas, capacity):
    partial_sum = lax.psum_scatter(
        sums,
        "tp",
        scatter_dimension=0,
        tiled=True,
    ).astype(jnp.float32)
    arrived = lax.all_to_all(
        partial_sum.reshape(local_width, -1, capacity).astype(jnp.bfloat16),
        "ep",
        split_axis=1,
        concat_axis=1,
        tiled=True,
    ).astype(jnp.float32)
    grouped = arrived.reshape(local_width, EXPERTS, replicas, capacity)
    return jnp.sum(grouped, axis=2).reshape(local_width, EXPERTS * capacity)


def per_device(
    tokens, expert_ids, route_share, w_gate, w_up, w_down, reward_head, upstream, pair_order
):
    tok_count, local_width = tokens.shape
    capacity = tok_count * expert_ids.shape[1] // EXPERTS
    n_ep = lax.axis_size("ep")
    replicas = n_ep // EXPERTS
    seq_local = tok_count // SEQ_LEN
    seq_total = pair_order.shape[0]
    seq_scale = loss_scale / math.sqrt(SEQ_LEN)
    picker, mixing = route_tables(expert_ids, route_share, capacity)
    tok_buf = slot_buffer(picker, tokens, capacity)
    ups_buf = slot_buffer(picker, upstream, capacity)
    seq_share = jnp.sum(mixing.reshape(seq_local, SEQ_LEN, EXPERTS, capacity), axis=1)
    meta = jnp.zeros((EXPERTS, 8 * pl.cdiv(seq_local, 8), 128 * pl.cdiv(capacity, 128)), jnp.float32)
    meta = meta.at[:, :seq_local, :capacity].set(seq_share.transpose(1, 0, 2))
    slot_rows, ups_part, meta_all, head_all = spread_slots(
        tok_buf, ups_buf, meta, reward_head.reshape(-1, 128)
    )
    width = slot_rows.shape[2]
    slot_rows = slot_rows.reshape(-1, width)
    ups_rows = lax.all_gather(ups_part, "tp", axis=2, tiled=True).reshape(-1, width)
    head_full = head_all.reshape(width)
    slot_meta = meta_all[:, :seq_local, :capacity]

    rows_by_cols = (((1,), (1,)), ((), ()))
    gate_pre = lax.dot_general(slot_rows, w_gate, rows_by_cols, preferred_element_type=jnp.float32)
    up_pre = lax.dot_general(slot_rows, w_up, rows_by_cols, preferred_element_type=jnp.float32)
    silu_value, silu_slope = silu_parts(gate_pre)
    hidden = (silu_value * up_pre).astype(jnp.bfloat16)

    def down_term(first_row, row_count):
        return lax.dot_general(
            w_down, hidden, (((0,), (1,)), ((), ())), preferred_element_type=jnp.float32
        )

    down_sums = down_term(0, 0).astype(jnp.bfloat16)
    down_sums, ups_rows, head_full = lax.optimization_barrier((down_sums, ups_rows, head_full))
    expert_sums = return_sums(down_sums, local_width, replicas, capacity)

    ups_cols = lax.dot_general(ups_rows, w_down, rows_by_cols, preferred_element_type=jnp.float32)
    head_parts = []
    head_rest = head_full
    for _ in range(3):
        part = lax.reduce_precision(head_rest, 8, 7)
        head_parts.append(part.astype(jnp.bfloat16))
        head_rest = head_rest - part
    head_cols = jnp.sum(
        lax.dot_general(
            jnp.stack(head_parts), w_down, rows_by_cols, preferred_element_type=jnp.float32
        ),
        axis=0,
    )

    slot_scores = jnp.sum(hidden.astype(jnp.float32) * head_cols[None, :], axis=1)
    expert_part = jnp.sum(slot_meta * slot_scores.reshape(n_ep, 1, capacity), axis=2).reshape(-1)
    own_scores = jnp.sum(tokens.astype(jnp.float32) * reward_head[None, :], axis=1)
    own_part = jnp.sum(own_scores.reshape(seq_local, SEQ_LEN), axis=1)
    offset = lax.axis_index("ep") * seq_local
    placed = lax.dynamic_update_slice(jnp.zeros((seq_total,), jnp.float32), own_part, (offset,))
    lanes = 1024 * pl.cdiv(seq_total, 1024)
    mine = jnp.pad(placed + expert_part, (0, lanes - seq_total)).reshape(-1, 128)
    gathered = share_rows(mine)
    rewards = jnp.sum(gathered, axis=0).reshape(-1)[:seq_total] / math.sqrt(SEQ_LEN)

    seq_iota = jnp.arange(seq_total, dtype=jnp.int32)
    chosen_hot = (pair_order[0::2][:, None] == seq_iota[None, :]).astype(jnp.float32)
    rejected_hot = (pair_order[1::2][:, None] == seq_iota[None, :]).astype(jnp.float32)
    margin = jnp.sum((chosen_hot - rejected_hot) * rewards[None, :], axis=1)
    pair_loss = jnp.mean(jax.nn.softplus(-margin))
    pair_weight = jax.nn.sigmoid(-margin)
    seq_coef = jnp.sum(pair_weight[:, None] * (rejected_hot - chosen_hot), axis=0)
    token_coef = jnp.repeat(lax.dynamic_slice_in_dim(seq_coef, offset, seq_local), SEQ_LEN)
    grad_out = (
        upstream.astype(jnp.float32) + seq_scale * token_coef[:, None] * reward_head[None, :]
    ).astype(jnp.bfloat16)

    slot_share = jnp.sum(slot_meta, axis=1).reshape(-1, 1)
    coef_of = seq_coef.reshape(n_ep, seq_local, 1)
    slot_coef = seq_scale * jnp.sum(jnp.where(slot_meta > 0.0, coef_of, 0.0), axis=1).reshape(-1, 1)
    slot_out = (ups_rows.astype(jnp.float32) + slot_coef * head_full[None, :]).astype(jnp.bfloat16)
    grad_slots = (slot_share * slot_out.astype(jnp.float32)).astype(jnp.bfloat16)
    hidden_grad = slot_share * (ups_cols + slot_coef * head_cols[None, :])
    gate_grad = (hidden_grad * up_pre * silu_slope).astype(jnp.bfloat16)
    up_grad = (hidden_grad * silu_value).astype(jnp.bfloat16)

    def input_term(first_row, row_count):
        across = (((0,), (1,)), ((), ()))
        return lax.dot_general(
            w_gate, gate_grad, across, preferred_element_type=jnp.float32
        ) + lax.dot_general(w_up, up_grad, across, preferred_element_type=jnp.float32)

    term_sums = input_term(0, 0).astype(jnp.bfloat16)
    term_sums, gate_grad, up_grad, grad_slots = lax.optimization_barrier(
        (term_sums, gate_grad, up_grad, grad_slots)
    )
    input_sums = return_sums(term_sums, local_width, replicas, capacity)

    over_slots = (((0,), (0,)), ((), ()))
    grad_down = lax.dot_general(
        hidden, grad_slots, over_slots, preferred_element_type=jnp.float32
    ).astype(jnp.bfloat16)
    grad_gate = lax.dot_general(
        gate_grad, slot_rows, over_slots, preferred_element_type=jnp.float32
    ).astype(jnp.bfloat16)
    grad_up = lax.dot_general(
        up_grad, slot_rows, over_slots, preferred_element_type=jnp.float32
    ).astype(jnp.bfloat16)

    mixed_sum = lax.dot_general(
        mixing, expert_sums, rows_by_cols, precision=highest, preferred_element_type=jnp.float32
    )
    layer_out = (tokens.astype(jnp.float32) + mixed_sum).astype(jnp.bfloat16)
    returned = lax.dot_general(
        picker, input_sums, rows_by_cols, precision=highest, preferred_element_type=jnp.float32
    )
    grad_tokens = (grad_out.astype(jnp.float32) + returned).astype(jnp.bfloat16)
    return (layer_out, rewards, pair_loss, grad_tokens, grad_gate, grad_up, grad_down)


def solution(mesh):
    in_specs = (
        P("ep", "tp"),
        P("ep", None),
        P("ep"),
        P(("ep", "tp"), None),
        P(("ep", "tp"), None),
        P(("ep", "tp"), None),
        P("tp"),
        P("ep", "tp"),
        P(),
    )
    out_specs = (
        P("ep", "tp"),
        P(),
        P(),
        P("ep", "tp"),
        P(("ep", "tp"), None),
        P(("ep", "tp"), None),
        P(("ep", "tp"), None),
    )
    return jax.shard_map(
        per_device, mesh=mesh, in_specs=in_specs, out_specs=out_specs, check_vma=False
    )
```

profile of v0, /device:TPU:0, one launch (start us, length us, event | category | flops | bytes accessed | tf_op | source)
XLA Modules:
  0.0 179.5 jit_solution(2102578063148248935)
XLA Ops:
  7.2 0.8 subtract_bitcast_fusion
  8.0 0.8 slice_bitcast_fusion.1
  8.7 0.1 fusion.8
  8.9 0.2 reduce_window_sum.18
  9.0 0.2 reduce_window_sum.17
  9.2 0.2 select_reduce_fusion.2
  9.4 0.2 select_reduce_fusion.1
  9.6 0.7 add_select_fusion
  10.3 0.7 maximum_select_fusion
  10.9 0.1 convert_reduce_fusion
  11.2 0.2 reshape.177
  11.4 0.3 reduce_sum.166
  11.7 0.1 copy.24
  11.8 0.6 scatter.4.meta_ref
  12.5 1.0 convolution_convert_fusion.4
  13.5 1.0 convolution_convert_fusion.5
  14.6 25.3 %spread_slots.1 = (bf16[8,32,3072]{2,1,0:T(8,128)(2,1)}, bf16[8,32,768]{2,1,0:T(8,128)(2,1)}, f32[8,8,128]{2,1,0:T(8,128)}, f32[4,6,128]{2,1,0:T(8,128)}) custom-call(bf16[8,32,768]{2,1,0:T(8,128)(2,1)} %bitcast.60, bf16[8,32,768]{2,1,0:T(8,128)(2,1)} %bitcast.59, f32[8,8,128]{2,1,0:T(8,128)} %scatter.4.meta_ref, f32[6,128]{1,0:T(8,128)} %bitcast.65), custom_call_target="tpu_custom_call" | custom-call | tf_op jit(solution)/shard_map/spread_slots/pallas_call | solution.py:179
  40.0 0.1 slice.48
  40.1 0.1 slice.47
  40.2 9.9 %fusion.27 = f32[256,2048]{1,0:T(8,128)} fusion(bf16[256,3072]{1,0:T(8,128)(2,1)} %bitcast.53, bf16[2048,3072]{1,0:T(8,128)(2,1)} %param.14), kind=kOutput, calls=%fused_computation.79 | convolution fusion | flops 3221225472 | bytes 16252928 | tf_op jit(solution)/shard_map/dot_general | solution.py:291
  50.1 0.1 fusion.7
  50.3 0.1 reduce_sum.171
  50.5 14.9 %multiply_convert_fusion.3 = (bf16[256,2048]{1,0:T(8,128)(2,1)S(1)}, f32[256,2048]{1,0:T(8,128)}) fusion(f32[256,2048]{1,0:T(8,128)} %fusion.27, bf16[256,3072]{1,0:T(8,128)(2,1)S(1)} %bitcast.54, bf16[2048,3072]{1,0:T(8,128)(2,1)} %param.15), kind=kOutput, calls=%fused_computation.15 | convolution fusion | flops 3224371200 | bytes 19398656 | tf_op jit(solution)/shard_map/dot_general | solution.py:292
  65.4 9.4 %fusion.1 = bf16[3072,256]{0,1:T(8,128)(2,1)} fusion(bf16[256,2048]{1,0:T(8,128)(2,1)S(1)} %get-tuple-element.56, bf16[2048,3072]{1,0:T(8,128)(2,1)} %param.16), kind=kOutput, calls=%fused_computation.6 | convolution fusion | flops 3222011904 | bytes 15204352 | tf_op jit(solution)/shard_map/dot_general | solution.py:297
  74.9 0.2 reduce-scatter.5.cloned.1.call-start
  75.2 7.9 %convolution_reduce_fusion = f32[2048]{0:T(1024)S(1)} fusion(bf16[2048,3072]{1,0:T(8,128)(2,1)} %param.16, bf16[1,3072]{1,0:T(2,128)(2,1)S(1)} %stack.38, bf16[1,3072]{1,0:T(2,128)(2,1)S(1)} %stack.37, bf16[1,3072]{1,0:T(2,128)(2,1)S(1)} %stack.36), kind=kOutput, calls=%fused_computation.24 | convolution fusion | flops 37808128 | bytes 12609536 | tf_op jit(solution)/shard_map/dot_general | solution.py:313
  83.1 0.3 multiply_reduce_fusion
  83.7 0.2 add_dynamic-update-slice_fusion
  83.8 0.6 pad_bitcast_fusion.mine_ref
  84.4 13.2 %share_rows.1 = f32[32,8,128]{2,1,0:T(8,128)} custom-call(f32[8,128]{1,0:T(8,128)} %pad_bitcast_fusion.mine_ref), custom_call_target="tpu_custom_call" | custom-call | tf_op jit(solution)/shard_map/share_rows/pallas_call | solution.py:236
  97.6 0.9 reduce_sum.172
  98.6 0.2 fusion.22
  98.7 0.6 add_divide_fusion.1
  99.4 0.1 fusion.24
  99.8 10.6 %multiply_convert_fusion.1 = (bf16[256,2048]{1,0:T(8,128)(2,1)S(1)}, bf16[256,2048]{1,0:T(8,128)(2,1)S(1)}) fusion(f32[256,2048]{1,0:T(8,128)} %fusion.27, f32[256,2048]{1,0:T(8,128)} %get-tuple-element.57, f32[2048]{0:T(1024)S(1)} %convolution_reduce_fusion, f32[256]{0:T(256)S(1)} %mul.197, bf16[256,3072]{1,0:T(8,128)(2,1)} %bitcast.61, ...), kind=kOutput, calls=%fused_computation.12 | convolution fusion | flops 3229614080 | bytes 20457472 | tf_op jit(solution)/shard_map/dot_general | solution.py:305
  110.5 0.7 multiply_convert_fusion
  111.3 7.4 %fusion.28 = f32[256,3072]{1,0:T(8,128)S(1)} fusion(bf16[256,2048]{1,0:T(8,128)(2,1)S(1)} %get-tuple-element.38, bf16[2048,3072]{1,0:T(8,128)(2,1)} %param.14), kind=kOutput, calls=%fused_computation.80 | convolution fusion | flops 3221225472 | bytes 16777216 | tf_op jit(solution)/shard_map/dot_general | solution.py:353
  118.7 0.8 slice-done.2
  119.5 4.6 %fusion.2 = bf16[3072,256]{0,1:T(8,128)(2,1)} fusion(f32[256,3072]{1,0:T(8,128)S(1)} %fusion.28, bf16[256,2048]{1,0:T(8,128)(2,1)S(1)} %get-tuple-element.39, bf16[2048,3072]{1,0:T(8,128)(2,1)S(1)} %bitcast.74), kind=kOutput, calls=%fused_computation.7 | convolution fusion | flops 3222798336 | bytes 18350080 | tf_op jit(solution)/shard_map/dot_general | solution.py:355
  124.1 7.9 %convolution_convert_fusion = bf16[2048,3072]{1,0:T(8,128)(2,1)} fusion(bf16[256,2048]{1,0:T(8,128)(2,1)} %copy-done.1, bf16[256,3072]{1,0:T(8,128)(2,1)S(1)} %multiply_convert_fusion), kind=kOutput, calls=%fused_computation | convolution fusion | flops 3227516928 | bytes 15204352 | tf_op jit(solution)/shard_map/dot_general | solution.py:364
  132.0 5.9 %all-to-all-start = ((bf16[768,8,32]{0,2,1:T(8,128)(2,1)}), bf16[768,8,32]{0,2,1:T(8,128)(2,1)S(1)}, u32[]{:S(2)}, u32[]{:S(2)}) async-start(bf16[768,8,32]{0,2,1:T(8,128)(2,1)} %bitcast.63), calls=%async_computation.1 | async-start | bytes 786432 | tf_op jit(solution)/shard_map/all_to_all | solution.py:254
  137.9 7.8 %convolution_convert_fusion.2 = bf16[2048,3072]{1,0:T(8,128)(2,1)} fusion(bf16[256,2048]{1,0:T(8,128)(2,1)} %copy-done.5, bf16[256,3072]{1,0:T(8,128)(2,1)S(1)} %bitcast.55), kind=kOutput, calls=%fused_computation.2 | convolution fusion | flops 3227516928 | bytes 15204352 | tf_op jit(solution)/shard_map/dot_general | solution.py:367
  145.7 8.1 %reduce-scatter.5.cloned.1.call-done = bf16[768,256]{0,1:T(8,128)(2,1)} async-done(((bf16[3072,256]{0,1:T(8,128)(2,1)}), bf16[768,256]{0,1:T(8,128)(2,1)}) %reduce-scatter.5.cloned.1.call-update) | async-done | bytes 393232 | tf_op jit(solution)/shard_map/reduce_scatter | solution.py:248
  153.8 5.5 %all-to-all-start.1 = ((bf16[768,8,32]{0,2,1:T(8,128)(2,1)}), bf16[768,8,32]{0,2,1:T(8,128)(2,1)S(1)}, u32[]{:S(2)}, u32[]{:S(2)}) async-start(bf16[768,8,32]{0,2,1:T(8,128)(2,1)} %bitcast.64), calls=%async_computation.3 | async-start | bytes 786432 | tf_op jit(solution)/shard_map/all_to_all | solution.py:254
  159.3 7.9 %convolution_convert_fusion.1 = bf16[2048,3072]{1,0:T(8,128)(2,1)} fusion(bf16[256,2048]{1,0:T(8,128)(2,1)} %copy-done.4, bf16[256,3072]{1,0:T(8,128)(2,1)S(1)} %bitcast.56), kind=kOutput, calls=%fused_computation.1 | convolution fusion | flops 3227516928 | bytes 15204352 | tf_op jit(solution)/shard_map/dot_general | solution.py:370
  168.1 1.0 fusion.5
  169.2 1.7 all-to-all-done.1
  170.9 1.0 fusion.6
  (63 shorter events, 1.3 us)
Async XLA Ops:
  7.2 5.3 %copy-start.8 = (bf16[128,768]{1,0:T(8,128)(2,1)S(1)}, bf16[128,768]{1,0:T(8,128)(2,1)}, u32[]{:S(2)}) copy-start(bf16[128,768]{1,0:T(8,128)(2,1)} %param.18) | copy-start | bytes 589828
  7.2 6.3 %copy-start.2 = (bf16[128,768]{1,0:T(8,128)(2,1)S(1)}, bf16[128,768]{1,0:T(8,128)(2,1)}, u32[]{:S(2)}) copy-start(bf16[128,768]{1,0:T(8,128)(2,1)} %param.11) | copy-start | bytes 589828
  7.2 67.7 %all-gather.2.cloned.1.call-start = ((), (), s32[]{:S(2)}) async-start(), calls=%async_computation.4 | async-start | bytes 1966080 | tf_op jit(solution)/shard_map/all_gather | solution.py:286
  9.6 30.4 %copy-start.14 = (s32[16]{0:T(128)S(1)}, s32[16]{0:T(128)}, u32[]{:S(2)}) copy-start(s32[16]{0:T(128)} %param.19) | copy-start | bytes 196
  11.1 29.1 %copy-start.6 = (f32[128,256]{1,0:T(8,128)}, f32[128,256]{1,0:T(8,128)S(1)}, u32[]{:S(2)}) copy-start(f32[128,256]{1,0:T(8,128)S(1)} %get-tuple-element.44) | copy-start | bytes 393220
  39.9 92.1 %reduce-scatter.3.cloned.1.call-start = ((), (), s32[]{:S(2)}) async-start(), calls=%async_computation.5 | async-start | bytes 1966080 | tf_op jit(solution)/shard_map/reduce_scatter | solution.py:248
  40.2 10.0 %copy-start.10 = (f32[768]{0:T(1024)S(1)}, f32[768]{0:T(1024)}, u32[]{:S(2)}) copy-start(f32[768]{0:T(1024)} %param.17) | copy-start | bytes 9220
  40.2 10.3 %copy-start.11 = (f32[4,6,128]{2,1,0:T(8,128)S(1)}, f32[4,6,128]{2,1,0:T(8,128)}, u32[]{:S(2)}) copy-start(f32[4,6,128]{2,1,0:T(8,128)} %get-tuple-element.32) | copy-start | bytes 36868
  40.2 10.3 %copy-start = (bf16[8,32,3072]{2,1,0:T(8,128)(2,1)S(1)}, bf16[8,32,3072]{2,1,0:T(8,128)(2,1)}, u32[]{:S(2)}) copy-start(bf16[8,32,3072]{2,1,0:T(8,128)(2,1)} %get-tuple-element.30) | copy-start | bytes 4718596
  65.4 17.7 %copy-start.1 = (bf16[256,2048]{1,0:T(8,128)(2,1)}, bf16[256,2048]{1,0:T(8,128)(2,1)S(1)}, u32[]{:S(2)}) copy-start(bf16[256,2048]{1,0:T(8,128)(2,1)S(1)} %get-tuple-element.56) | copy-start | bytes 3145732
  74.9 78.9 %reduce-scatter.5.cloned.1.call-start = ((), (), s32[]{:S(2)}) async-start(), calls=%async_computation.6 | async-start | bytes 1966080 | tf_op jit(solution)/shard_map/reduce_scatter | solution.py:248
  75.2 8.3 %copy-start.12 = (f32[8,8,128]{2,1,0:T(8,128)S(1)}, f32[8,8,128]{2,1,0:T(8,128)}, u32[]{:S(2)}) copy-start(f32[8,8,128]{2,1,0:T(8,128)} %get-tuple-element.34) | copy-start | bytes 98308
  98.6 11.9 %copy-start.13 = (f32[16]{0:T(128)}, f32[16]{0:T(128)S(1)}, u32[]{:S(2)}) copy-start(f32[16]{0:T(128)S(1)} %slice_multiply_fusion) | copy-start | bytes 196
  99.8 10.6 %copy-start.3 = (bf16[8,32,3072]{2,1,0:T(8,128)(2,1)S(1)}, bf16[8,32,3072]{2,1,0:T(8,128)(2,1)}, u32[]{:S(2)}) copy-start(bf16[8,32,3072]{2,1,0:T(8,128)(2,1)} %all-gather.2.cloned.1.call-done) | copy-start | bytes 4718596
  110.5 8.2 %copy-start.5 = (bf16[256,2048]{1,0:T(8,128)(2,1)}, bf16[256,2048]{1,0:T(8,128)(2,1)S(1)}, u32[]{:S(2)}) copy-start(bf16[256,2048]{1,0:T(8,128)(2,1)S(1)} %get-tuple-element.38) | copy-start | bytes 3145732
  110.5 8.2 %copy-start.4 = (bf16[256,2048]{1,0:T(8,128)(2,1)}, bf16[256,2048]{1,0:T(8,128)(2,1)S(1)}, u32[]{:S(2)}) copy-start(bf16[256,2048]{1,0:T(8,128)(2,1)S(1)} %get-tuple-element.39) | copy-start | bytes 3145732
  110.5 8.2 %slice-start = ((s8[12582912]{0:T(1024)(128)(4,1)}), s8[4194304]{0:T(1024)(128)(4,1)S(1)}, s32[]{:S(2)}) async-start(s8[12582912]{0:T(1024)(128)(4,1)} %bitcast.73), calls=%async_computation.7 | async-start | bytes 8388608
  111.2 7.5 %slice-start.1 = ((s8[12582912]{0:T(1024)(128)(4,1)}), s8[4194304]{0:T(1024)(128)(4,1)S(1)}, s32[]{:S(2)}) async-start(s8[12582912]{0:T(1024)(128)(4,1)} %bitcast.73), calls=%async_computation.8 | async-start | bytes 8388608
  111.3 8.2 %slice-start.2 = ((s8[12582912]{0:T(1024)(128)(4,1)}), s8[4194304]{0:T(1024)(128)(4,1)S(1)}, s32[]{:S(2)}) async-start(s8[12582912]{0:T(1024)(128)(4,1)} %bitcast.73), calls=%async_computation.9 | async-start | bytes 8388608
  132.0 21.8 %all-to-all-start = ((bf16[768,8,32]{0,2,1:T(8,128)(2,1)}), bf16[768,8,32]{0,2,1:T(8,128)(2,1)S(1)}, u32[]{:S(2)}, u32[]{:S(2)}) async-start(bf16[768,8,32]{0,2,1:T(8,128)(2,1)} %bitcast.63), calls=%async_computation.1 | async-start | bytes 786432 | tf_op jit(solution)/shard_map/all_to_all | solution.py:254
  153.8 17.0 %all-to-all-start.1 = ((bf16[768,8,32]{0,2,1:T(8,128)(2,1)}), bf16[768,8,32]{0,2,1:T(8,128)(2,1)S(1)}, u32[]{:S(2)}, u32[]{:S(2)}) async-start(bf16[768,8,32]{0,2,1:T(8,128)(2,1)} %bitcast.64), calls=%async_computation.3 | async-start | bytes 786432 | tf_op jit(solution)/shard_map/all_to_all | solution.py:254
  159.3 8.8 %copy-start.7 = (f32[128,256]{1,0:T(8,128)S(1)}, f32[128,256]{1,0:T(8,128)}, u32[]{:S(2)}) copy-start(f32[128,256]{1,0:T(8,128)} %copy-done.6) | copy-start | bytes 393220
  159.3 11.5 %copy-start.9 = (bf16[128,768]{1,0:T(8,128)(2,1)S(1)}, bf16[128,768]{1,0:T(8,128)(2,1)}, u32[]{:S(2)}) copy-start(bf16[128,768]{1,0:T(8,128)(2,1)} %param.18) | copy-start | bytes 589828
Sparse Core Ops, SparseCore 0:
  40.0 24.5 all-gather.1
  75.0 32.6 reduce-scatter.2
  124.2 29.5 reduce-scatter.4
where the time goes:
time: 180 us
  matrix products  92.6 us (51%)
  Pallas kernels  38.5 us (21%)
  between operations  15.9 us (9%)
  starting transfers between devices  11.7 us (6%)
  waiting for transfers between devices  9.82 us (5%)
  other arithmetic  6.94 us (4%)
  local copies, waits for them, and re-layouts  4.14 us (2%)
    pallas_call x1, Pallas kernels, spread_slots(): pl.pallas_call(partial(spread_kernel, n_ep, n_tp), out_shape=(jax.ShapeDt...  25.3 us
    dot_general x1, matrix products, per_device(): lax.dot_general(slot_rows, w_up, rows_by_cols, preferred_element_type=jnp...  14.9 us
    pallas_call x1, Pallas kernels, share_rows(): pl.pallas_call(partial(share_kernel, n_ep, n_tp), out_shape=jax.ShapeDtyp...  13.2 us
    all_to_all x2, starting transfers between devices, return_sums(): lax.all_to_all(partial_sum.reshape(local_width, -1, capacity).astype(jnp....  11.4 us
    dot_general x1, matrix products, per_device(): lax.dot_general(ups_rows, w_down, rows_by_cols, preferred_element_type=jn...  10.6 us
    dot_general x1, matrix products, per_device(): lax.dot_general(slot_rows, w_gate, rows_by_cols, preferred_element_type=j...  9.93 us
    dot_general x1, matrix products, down_term(): lax.dot_general(w_down, hidden, (((0,), (1,)), ((), ())), preferred_eleme...  9.44 us
    reduce_scatter x2, waiting for transfers between devices, return_sums(): lax.psum_scatter(sums, 'tp', scatter_dimension=0, tiled=True)  8.07 us
  transfers between devices with their start and end apart: 5, of which 2 were waited for; matrix products, arithmetic and copies ran while one was open for 53% of the time, Pallas kernels for 7%

commit v1 on v0

v1 whole, which is shorter than its diff:
```python
import math
from functools import partial

import jax
import jax.numpy as jnp
from jax import lax
from jax.experimental import pallas as pl
from jax.experimental.pallas import tpu as pltpu
from jax.sharding import PartitionSpec as P

EXPERTS = 8
SEQ_LEN = 64

loss_scale = 256.0
MESH = pl.DeviceIdType.MESH
NT = (((1,), (1,)), ((), ()))
NN = (((1,), (0,)), ((), ()))
f32 = jnp.float32
bf16 = jnp.bfloat16


def dot(a, b, dims=NN):
    return lax.dot_general(a, b, dims, preferred_element_type=f32)


def remote(src, dst, send_sem, recv_sem, target):
    return pltpu.make_async_remote_copy(
        src_ref=src,
        dst_ref=dst,
        send_sem=send_sem,
        recv_sem=recv_sem,
        device_id=target,
        device_id_type=MESH,
    )


def drain(sent, sem):
    pltpu.make_async_copy(sent, sent, sem).wait()


def layer_kernel(
    n_ep, n_tp, chunks,
    pack_ref, tok_ref, ups_ref, head_ref, pair_ref, wg_ref, wu_ref, wd_ref,
    slots_ref, gslot_ref, hid_ref, gg_ref, ug_ref, layer_ref, gtok_ref, rew_ref, loss_ref,
    wg_v, wu_v, wd_v, tokb, upsb, raw_all, head_all, hp, hc, mixing, picks, meta, meta_t,
    act_a, act_b, uc, rows_a, rows_b, scores, own_row, all_rows, share_row, coef_row, coef_col,
    part_d, pair_d, ybuf_d, sums_d, part_i, pair_i, ybuf_i, sums_i,
    w_sem, local_sem, a2a_send, tok_recv, ups_recv, raw_send, raw_recv, head_send, head_recv,
    tok_tp_send, tok_tp_recv, ups_tp_send, ups_tp_recv, rew_send, rew_recv,
    pair_send, pair_recv_d, pair_recv_i, y_send, y_recv_d, y_recv_i, z_send, z_recv_d, z_recv_i,
):
    q = lax.axis_index("ep")
    t = lax.axis_index("tp")
    count = n_ep * n_tp
    me = q * n_tp + t
    n_y = n_tp // 2
    y = t // 2
    core = t % 2
    partner = y * 2 + 1 - core
    tokens, width = tok_ref.shape
    cap = tokb.shape[1]
    replicas = n_ep // EXPERTS
    depth = slots_ref.shape[2]
    rows = n_ep * cap
    ff = wg_v.shape[0]
    fc = ff // chunks
    per = n_ep // chunks
    lanes = meta.shape[1]
    seq_local = tokens // SEQ_LEN
    seq_scale = loss_scale / math.sqrt(SEQ_LEN)
    expert = q // replicas

    def chunk(c):
        return pl.ds(pl.multiple_of(c * fc, fc), fc)

    def load(c, i, src, dst):
        return pltpu.make_async_copy(src.at[chunk(c)], dst.at[chunk(c)], w_sem.at[i, c])

    for i, (src, dst) in enumerate(((wd_ref, wd_v), (wg_ref, wg_v), (wu_ref, wu_v))):
        for c in range(chunks):
            load(c, i, src, dst).start()

    barrier = pltpu.get_barrier_semaphore()

    def greet(k, carry):
        other = (me + k) % count
        pl.semaphore_signal(
            barrier, inc=1, device_id=(other // n_tp, other % n_tp), device_id_type=MESH
        )
        return carry

    lax.fori_loop(1, count, greet, 0)

    before = (
        lax.broadcasted_iota(jnp.int32, (tokens, tokens), 0)
        < lax.broadcasted_iota(jnp.int32, (tokens, tokens), 1)
    ).astype(f32).astype(bf16)

    def places(first_id, second_id, wanted):
        first = (first_id == wanted).astype(f32)
        second = (second_id == wanted).astype(f32)
        first_rank = dot(first.astype(bf16), before)
        second_rank = dot(second.astype(bf16), before) + jnp.sum(first, axis=1, keepdims=True)
        return first, first_rank, second, second_rank

    experts_iota = lax.broadcasted_iota(jnp.int32, (EXPERTS, tokens), 0).astype(f32)
    pack = pack_ref[...]
    first_id, second_id, share = pack[0:1], pack[1:2], pack[2:3]
    first, first_rank, second, second_rank = places(first_id, second_id, experts_iota)

    def slot_of(hot, rank, ids):
        own_rank = jnp.sum(hot * rank, axis=0, keepdims=True)
        return jnp.where(own_rank < cap, ids * cap + own_rank, -1.0)

    first_slot = slot_of(first, first_rank, first_id)
    second_slot = slot_of(second, second_rank, second_id)
    slot_iota = lax.broadcasted_iota(jnp.int32, (EXPERTS * cap, tokens), 0).astype(f32)
    take = ((slot_iota == first_slot) | (slot_iota == second_slot)).astype(f32).astype(bf16)
    tokb[...] = dot(take, tok_ref[...]).astype(bf16).reshape(EXPERTS, cap, width)
    upsb[...] = dot(take, ups_ref[...]).astype(bf16).reshape(EXPERTS, cap, width)
    pl.semaphore_wait(barrier, count - 1)

    def columns(owner):
        return pl.ds(pl.multiple_of(owner * width, 128), width)

    own = q // replicas
    own_tok = pltpu.make_async_copy(tokb.at[own], slots_ref.at[q, :, columns(t)], local_sem.at[0])
    own_ups = pltpu.make_async_copy(upsb.at[own], gslot_ref.at[q, :, columns(t)], local_sem.at[1])
    own_raw = pltpu.make_async_copy(pack_ref, raw_all.at[q], local_sem.at[2])
    own_head = pltpu.make_async_copy(head_ref, head_all.at[t], local_sem.at[3])

    def spread(buf, out, recv, k):
        to = (q + k) % n_ep
        return remote(
            buf.at[to // replicas], out.at[q, :, columns(t)], a2a_send, recv.at[k], (to, t)
        )

    def arrive(buf, out, recv, k):
        source = (q + n_ep - k) % n_ep
        remote(
            buf.at[0], out.at[source, :, columns(t)], a2a_send, recv.at[k], (source, t)
        ).wait_recv()

    for copy in (own_tok, own_head, own_raw, own_ups):
        copy.start()
    for k in range(1, n_tp):
        remote(
            head_ref, head_all.at[t], head_send, head_recv.at[k], (q, (t + k) % n_tp)
        ).start()

    def send_tok(k, carry):
        spread(tokb, slots_ref, tok_recv, k).start()
        return carry

    lax.fori_loop(1, n_ep, send_tok, 0)

    def send_raw(k, carry):
        to = (q + k) % n_ep
        remote(pack_ref, raw_all.at[q], raw_send, raw_recv.at[k], (to, t)).start()
        return carry

    lax.fori_loop(1, n_ep, send_raw, 0)

    def hand_on(out, sems, k, owner, target, row):
        send, recv = sems
        piece = out.at[(q + n_ep - k) % n_ep, :, columns(owner)]
        return remote(piece, piece, send, recv.at[row, k], (q, target))

    def pass_on(out, sems, k):
        for j in range(1, n_y):
            hand_on(out, sems, k, t, (t + 2 * j) % n_tp, j - 1).start()
        hand_on(out, sems, k, t, partner, n_y - 1).start()

    def forward(out, sems, k):
        for j in range(1, n_y):
            origin = (t + n_tp - 2 * j) % n_tp
            hand_on(out, sems, k, origin, t, j - 1).wait_recv()
            hand_on(out, sems, k, origin, partner, n_y - 1 + j).start()

    def finish(out, sems):
        def one(k, carry):
            hand_on(out, sems, k, partner, t, n_y - 1).wait_recv()
            for j in range(1, n_y):
                origin = (partner + n_tp - 2 * j) % n_tp
                hand_on(out, sems, k, origin, t, n_y - 1 + j).wait_recv()
            return carry

        lax.fori_loop(0, n_ep, one, 0)

    lag = min(2, n_ep)
    tok_sems = (tok_tp_send, tok_tp_recv)
    ups_sems = (ups_tp_send, ups_tp_recv)

    def step_piece(buf, out, recv, sems, own_copy, k):
        @pl.when(k == 0)
        def _():
            own_copy.wait()

        @pl.when(k > 0)
        def _():
            arrive(buf, out, recv, k)

        pass_on(out, sems, k)

        @pl.when(k >= lag)
        def _():
            forward(out, sems, k - lag)

    def last_pieces(out, sems):
        for k in range(n_ep - lag, n_ep):
            forward(out, sems, k)

    own_head.wait()
    tok_f = tok_ref[...].astype(f32)
    head_mine = head_ref[0:1, :]
    own_scores = jnp.sum(tok_f * head_mine, axis=1, keepdims=True)
    token_iota = lax.broadcasted_iota(jnp.int32, (tokens, lanes), 0)
    lane_iota = lax.broadcasted_iota(jnp.int32, (tokens, lanes), 1)
    token_seq = token_iota // SEQ_LEN + q * seq_local
    in_seq = token_seq == lane_iota
    own_row[...] = jnp.broadcast_to(
        jnp.sum(jnp.where(in_seq, own_scores, 0.0), axis=0, keepdims=True), own_row.shape
    )

    back_iota = lax.broadcasted_iota(jnp.int32, (rows, tokens), 0)
    back_slot = ((back_iota // (replicas * cap)) * cap + back_iota % cap).astype(f32)
    is_first = back_slot == first_slot
    is_second = back_slot == second_slot
    mix_t = jnp.where(is_first, share, 0.0) + jnp.where(is_second, 1.0 - share, 0.0)
    mixing[...] = mix_t.T
    picks[...] = (is_first | is_second).astype(f32).T.astype(bf16)

    for k in range(1, n_tp):
        source = (t + n_tp - k) % n_tp
        remote(head_ref, head_all.at[source], head_send, head_recv.at[k], (q, source)).wait_recv()
    part_iota = lax.broadcasted_iota(jnp.int32, (hp.shape[0], width), 0)
    for owner in range(n_tp):
        rest = head_all[owner][0:1, :]
        stacked = jnp.zeros((hp.shape[0], width), f32)
        for i in range(3):
            piece = rest.astype(bf16).astype(f32)
            stacked = jnp.where(part_iota == i, piece, stacked)
            rest = rest - piece
        hp[:, owner * width : (owner + 1) * width] = stacked.astype(bf16)

    def token_phase(c, carry):
        for j in range(per):
            k = c * per + j
            step_piece(tokb, slots_ref, tok_recv, tok_sems, own_tok, k)

            @pl.when(k > 0)
            def _():
                spread(upsb, gslot_ref, ups_recv, k).start()

        load(c, 0, wd_ref, wd_v).wait()
        head_dot = dot(wd_v[chunk(c), :], hp[...], NT)
        hc[chunk(c), :] = jnp.broadcast_to(jnp.sum(head_dot, axis=1, keepdims=True), (fc, 128))
        return carry

    lax.fori_loop(0, chunks, token_phase, 0)
    last_pieces(slots_ref, tok_sems)

    own_raw.wait()

    def raw_wait(k, carry):
        source = (q + n_ep - k) % n_ep
        remote(pack_ref, raw_all.at[source], raw_send, raw_recv.at[k], (source, t)).wait_recv()
        return carry

    lax.fori_loop(1, n_ep, raw_wait, 0)
    cap_iota = lax.broadcasted_iota(jnp.int32, (cap, tokens), 0).astype(f32)
    cap_token = lax.broadcasted_iota(jnp.int32, (cap, tokens), 1) // SEQ_LEN
    cap_lane = lax.broadcasted_iota(jnp.int32, (cap, lanes), 1)
    expert_f = expert.astype(f32)

    def block_meta(b, carry):
        raw = raw_all[b]
        hot = (raw == expert_f).astype(f32)
        rank = dot(hot.astype(bf16), before)
        first_hot, second_hot = hot[0:1], hot[1:2]
        second_of = rank[1:2] + jnp.sum(first_hot, axis=1, keepdims=True)
        first_at = jnp.where((first_hot > 0.0) & (rank[0:1] < cap), rank[0:1], -1.0)
        second_at = jnp.where((second_hot > 0.0) & (second_of < cap), second_of, -1.0)
        share_b = raw[2:3]
        shares = jnp.where(cap_iota == first_at, share_b, 0.0) + jnp.where(
            cap_iota == second_at, 1.0 - share_b, 0.0
        )
        spreaded = jnp.zeros((cap, lanes), f32)
        for s in range(seq_local):
            column = jnp.sum(jnp.where(cap_token == s, shares, 0.0), axis=1, keepdims=True)
            spreaded = jnp.where(cap_lane == b * seq_local + s, column, spreaded)
        meta[pl.ds(pl.multiple_of(b * cap, cap), cap), :] = spreaded
        return carry

    lax.fori_loop(0, n_ep, block_meta, 0)
    meta_t[...] = meta[...].T
    share_row[...] = jnp.broadcast_to(
        jnp.sum(meta_t[...], axis=0, keepdims=True), share_row.shape
    )
    finish(slots_ref, tok_sems)

    scores[...] = jnp.zeros_like(scores)

    def forward_phase(c, carry):
        for j in range(per):
            step_piece(upsb, gslot_ref, ups_recv, ups_sems, own_ups, c * per + j)
        load(c, 1, wg_ref, wg_v).wait()
        load(c, 2, wu_ref, wu_v).wait()
        slot_rows = slots_ref[...].reshape(rows, depth)
        gate = dot(wg_v[chunk(c), :], slot_rows, NT)
        up = dot(wu_v[chunk(c), :], slot_rows, NT)
        sigmoid = jax.nn.sigmoid(gate)
        silu = gate * sigmoid
        act_b[chunk(c), :] = silu
        act_a[chunk(c), :] = up * (sigmoid * (1.0 + gate * (1.0 - sigmoid)))
        hidden = (silu * up).astype(bf16)
        hid_ref[chunk(c), :] = hidden
        hidden_f = hidden.astype(f32)
        rows_a[:, chunk(c)] = hidden_f.T.astype(bf16)
        scores[...] += jnp.sum(hidden_f * hc[chunk(c), 0:1], axis=0, keepdims=True)
        return carry

    lax.fori_loop(0, chunks, forward_phase, 0)
    last_pieces(gslot_ref, ups_sems)

    by_seq = jnp.sum(meta_t[...] * scores[0:1, :], axis=1, keepdims=True)
    mine = own_row[...] + jnp.broadcast_to(by_seq, (lanes, lanes)).T[0:8]
    all_rows[me] = mine

    def send_row(k, carry):
        other = (me + k) % count
        remote(
            all_rows.at[me], all_rows.at[me], rew_send, rew_recv, (other // n_tp, other % n_tp)
        ).start()
        return carry

    lax.fori_loop(1, count, send_row, 0)

    nb = 256 if width % 256 == 0 else 128

    def product(part, target, lefts, weights):
        def tile(n, carry):
            cols = pl.ds(pl.multiple_of(target * width + n * nb, 128), nb)
            total = dot(lefts[0][...], weights[0][:, cols])
            for left, weight in zip(lefts[1:], weights[1:]):
                total = total + dot(left[...], weight[:, cols])
            part[target, :, :, pl.ds(pl.multiple_of(n * nb, 128), nb)] = total.astype(
                bf16
            ).reshape(n_ep, cap, nb)
            return carry

        lax.fori_loop(0, width // nb, tile, 0)

    def to_pair(part, pair, recv, yy):
        return remote(
            part.at[yy * 2 + 1 - core], pair.at[yy], pair_send, recv.at[yy], (q, partner)
        )

    def from_pair(part, pair, recv, yy):
        remote(
            part.at[yy * 2 + core], pair.at[yy], pair_send, recv.at[yy], (q, partner)
        ).wait_recv()

    def over_y(part, pair, ybuf, recv, r, k):
        yy = (y + r) % n_y
        blk = (q + k) % n_ep
        here = part[yy * 2 + core, blk].astype(f32) + pair[yy, blk].astype(f32)
        part[yy * 2 + core, blk] = here.astype(bf16)
        remote(
            part.at[yy * 2 + core, blk], ybuf.at[y, blk], y_send, recv.at[r, k],
            (q, yy * 2 + core),
        ).start()

    def over_z(part, pair, ybuf, sums, y_recv, z_recv, k):
        blk = (q + k) % n_ep
        total = part[t, blk].astype(f32) + pair[y, blk].astype(f32)
        for r in range(1, n_y):
            source = (y + n_y - r) % n_y
            remote(
                part.at[t, blk], ybuf.at[source, blk], y_send, y_recv.at[r, k],
                (q, source * 2 + core),
            ).wait_recv()
            total = total + ybuf[source, blk].astype(f32)

        @pl.when(k == 0)
        def _():
            sums[q] = total.astype(bf16)

        @pl.when(k > 0)
        def _():
            part[t, blk] = total.astype(bf16)
            remote(
                part.at[t, blk], sums.at[q], z_send, z_recv.at[k], (blk, t)
            ).start()

    def all_back(part, sums, z_recv):
        def one(k, carry):
            source = (q + n_ep - k) % n_ep
            remote(
                part.at[t, 0], sums.at[source], z_send, z_recv.at[k], (source, t)
            ).wait_recv()
            return carry

        lax.fori_loop(1, n_ep, one, 0)

    def down_phase(j, carry):
        yy = (y + 1 + j) % n_y
        product(part_d, yy * 2 + 1 - core, (rows_a,), (wd_v,))
        to_pair(part_d, pair_d, pair_recv_d, yy).start()
        product(part_d, yy * 2 + core, (rows_a,), (wd_v,))
        return carry

    lax.fori_loop(0, n_y, down_phase, 0)
    for r in range(n_y):
        from_pair(part_d, pair_d, pair_recv_d, (y + r) % n_y)
    finish(gslot_ref, ups_sems)

    def upstream_phase(c, carry):
        for j in range(per):
            for r in range(1, n_y):
                over_y(part_d, pair_d, ybuf_d, y_recv_d, r, c * per + j)
        uc[chunk(c), :] = dot(wd_v[chunk(c), :], gslot_ref[...].reshape(rows, depth), NT)
        return carry

    lax.fori_loop(0, chunks, upstream_phase, 0)

    rest_rows = all_rows.at[pl.ds(0, count - 1)]
    pltpu.make_async_copy(rest_rows, rest_rows, rew_recv).wait()
    rewards = jnp.sum(all_rows[...], axis=0)[0:1] / math.sqrt(SEQ_LEN)
    rew_ref[...] = jnp.broadcast_to(rewards, rew_ref.shape)
    pairs = pair_ref.shape[0]
    pair_lane = lax.broadcasted_iota(jnp.int32, (pairs, lanes), 1)
    chosen = (pair_lane == pair_ref[:, 0:1]).astype(f32)
    rejected = (pair_lane == pair_ref[:, 1:2]).astype(f32)
    margin = jnp.sum((chosen - rejected) * rewards, axis=1, keepdims=True)
    losses = jnp.maximum(-margin, 0.0) + jnp.log1p(jnp.exp(-jnp.abs(margin)))
    loss_ref[...] = jnp.broadcast_to(
        jnp.sum(losses, axis=0, keepdims=True) / pairs, loss_ref.shape
    )
    pair_weight = jax.nn.sigmoid(-margin)
    seq_coef = jnp.sum(pair_weight * (rejected - chosen), axis=0, keepdims=True)
    slot_coef = seq_scale * jnp.sum(
        jnp.where(meta[...] > 0.0, seq_coef, 0.0), axis=1, keepdims=True
    )
    coef_wide = jnp.broadcast_to(slot_coef, coef_col.shape)
    coef_col[...] = coef_wide
    coef_row[...] = coef_wide.T[0:8]

    def gradient_phase(c, carry):
        for i in range(per):
            k = c * per + i
            over_z(
                part_d, pair_d, ybuf_d, sums_d, y_recv_d, z_recv_d, (k + 1) % n_ep
            )
        hidden_grad = share_row[0:1, :] * (
            uc[chunk(c), :] + coef_row[0:1, :] * hc[chunk(c), 0:1]
        )
        gate_grad = (hidden_grad * act_a[chunk(c), :]).astype(bf16)
        up_grad = (hidden_grad * act_b[chunk(c), :]).astype(bf16)
        gg_ref[chunk(c), :] = gate_grad
        ug_ref[chunk(c), :] = up_grad
        rows_a[:, chunk(c)] = gate_grad.astype(f32).T.astype(bf16)
        rows_b[:, chunk(c)] = up_grad.astype(f32).T.astype(bf16)
        return carry

    lax.fori_loop(0, chunks, gradient_phase, 0)

    def input_phase(j, carry):
        yy = (y + 1 + j) % n_y
        product(part_i, yy * 2 + 1 - core, (rows_a, rows_b), (wg_v, wu_v))
        to_pair(part_i, pair_i, pair_recv_i, yy).start()
        product(part_i, yy * 2 + core, (rows_a, rows_b), (wg_v, wu_v))
        from_pair(part_i, pair_i, pair_recv_i, yy)

        @pl.when(j < n_y - 1)
        def _():
            def one(k, carry_k):
                over_y(part_i, pair_i, ybuf_i, y_recv_i, j + 1, k)
                return carry_k

            lax.fori_loop(0, n_ep, one, 0)

        return carry

    lax.fori_loop(0, n_y, input_phase, 0)

    drain(gslot_ref.at[:, :, pl.ds(0, (n_tp - 1) * width)], ups_tp_send)

    def tail_phase(k, carry):
        row_at = pl.ds(pl.multiple_of(k * cap, cap), cap)
        coef_k = coef_col[row_at, 0:1]
        share_k = jnp.sum(meta[row_at, :], axis=1, keepdims=True)
        for owner in range(n_tp):
            cols = pl.ds(owner * width, width)
            head_k = head_all[owner][0:1, :]
            slot_out = (gslot_ref[k, :, cols].astype(f32) + coef_k * head_k).astype(bf16)
            gslot_ref[k, :, cols] = (share_k * slot_out.astype(f32)).astype(bf16)
        over_z(part_i, pair_i, ybuf_i, sums_i, y_recv_i, z_recv_i, (k + 1) % n_ep)
        return carry

    lax.fori_loop(0, n_ep, tail_phase, 0)

    all_back(part_d, sums_d, z_recv_d)
    rest = mixing[...]
    mixed = tok_ref[...].astype(f32)
    expert_sums = sums_d[...].reshape(rows, width)
    for _ in range(3):
        piece = rest.astype(bf16)
        mixed = mixed + dot(piece, expert_sums)
        rest = rest - piece.astype(f32)
    layer_ref[...] = mixed.astype(bf16)
    token_coef = jnp.sum(jnp.where(in_seq, seq_coef, 0.0), axis=1, keepdims=True)
    grad_out = (ups_ref[...].astype(f32) + seq_scale * token_coef * head_mine).astype(bf16)
    all_back(part_i, sums_i, z_recv_i)
    returned = dot(picks[...], sums_i[...].reshape(rows, width))
    gtok_ref[...] = (grad_out.astype(f32) + returned).astype(bf16)

    drain(sums_d.at[pl.ds(0, n_ep - 1)], a2a_send)
    drain(sums_d.at[pl.ds(0, n_ep - 1)], a2a_send)
    drain(raw_all.at[pl.ds(0, n_ep - 1)], raw_send)
    drain(head_all.at[pl.ds(0, n_tp - 1)], head_send)
    drain(slots_ref.at[:, :, pl.ds(0, (n_tp - 1) * width)], tok_tp_send)
    drain(rest_rows, rew_send)
    for _ in range(2):
        drain(pair_d, pair_send)
        if n_y > 1:
            drain(ybuf_d.at[pl.ds(0, n_y - 1)], y_send)
        drain(sums_d.at[pl.ds(0, n_ep - 1)], z_send)


def run_layer(pack, tokens, upstream, head_rows, pairs, w_gate, w_up, w_down, seq_total, cap):
    n_ep = lax.axis_size("ep")
    n_tp = lax.axis_size("tp")
    n_y = n_tp // 2
    tok_count, width = tokens.shape
    ff, depth = w_gate.shape
    rows = n_ep * cap
    chunks = math.gcd(ff // 256, n_ep)
    lanes = 128 * pl.cdiv(seq_total, 128)
    dma = pltpu.SemaphoreType.DMA
    vmem = pl.BlockSpec(memory_space=pltpu.VMEM)
    hbm = pl.BlockSpec(memory_space=pl.ANY)

    def shape(*dims, kind=bf16):
        return jax.ShapeDtypeStruct(dims, kind)

    def scratch(*dims, kind=bf16):
        return pltpu.VMEM(dims, kind)

    back = [
        scratch(n_tp, n_ep, cap, width), scratch(n_y, n_ep, cap, width),
        scratch(n_y, n_ep, cap, width), scratch(n_ep, cap, width),
    ]
    return pl.pallas_call(
        partial(layer_kernel, n_ep, n_tp, chunks),
        out_shape=(
            shape(n_ep, cap, depth), shape(n_ep, cap, depth),
            shape(ff, rows), shape(ff, rows), shape(ff, rows),
            shape(tok_count, width), shape(tok_count, width),
            shape(8, lanes, kind=f32), shape(8, 128, kind=f32),
        ),
        in_specs=[vmem] * 5 + [hbm] * 3,
        out_specs=[vmem] * 9,
        scratch_shapes=[
            scratch(ff, depth), scratch(ff, depth), scratch(ff, depth),
            scratch(EXPERTS, cap, width), scratch(EXPERTS, cap, width),
            scratch(n_ep, 8, tok_count, kind=f32), scratch(n_tp, 8, width, kind=f32),
            scratch(16, depth), scratch(ff, 128, kind=f32),
            scratch(tok_count, rows, kind=f32), scratch(tok_count, rows),
            scratch(rows, lanes, kind=f32), scratch(lanes, rows, kind=f32),
            scratch(ff, rows, kind=f32), scratch(ff, rows, kind=f32), scratch(ff, rows, kind=f32),
            scratch(rows, ff), scratch(rows, ff),
            scratch(8, rows, kind=f32), scratch(8, lanes, kind=f32),
            scratch(n_ep * n_tp, 8, lanes, kind=f32),
            scratch(8, rows, kind=f32), scratch(8, rows, kind=f32), scratch(rows, 128, kind=f32),
        ] + back + back + [
            dma((3, chunks)), dma((4,)), dma, dma((n_ep,)), dma((n_ep,)), dma, dma((n_ep,)),
            dma, dma((n_tp,)), dma, dma((n_tp - 1, n_ep)), dma, dma((n_tp - 1, n_ep)), dma, dma,
            dma, dma((n_y,)), dma((n_y,)), dma, dma((n_y, n_ep)), dma((n_y, n_ep)),
            dma, dma((n_ep,)), dma((n_ep,)),
        ],
        compiler_params=pltpu.CompilerParams(
            collective_id=0, has_side_effects=True, vmem_limit_bytes=67000000
        ),
        name="run_layer",
    )(pack, tokens, upstream, head_rows, pairs, w_gate, w_up, w_down)


def grads_kernel(hid_ref, gg_ref, ug_ref, slots_ref, gslot_ref, down_ref, gate_ref, up_ref):
    depth = slots_ref.shape[1]
    step = 512 if depth % 512 == 0 else 128

    def tile(n, carry):
        cols = pl.ds(pl.multiple_of(n * step, step), step)
        grads = gslot_ref[:, cols]
        inputs = slots_ref[:, cols]
        down_ref[:, cols] = dot(hid_ref[...], grads).astype(bf16)
        gate_ref[:, cols] = dot(gg_ref[...], inputs).astype(bf16)
        up_ref[:, cols] = dot(ug_ref[...], inputs).astype(bf16)
        return carry

    lax.fori_loop(0, depth // step, tile, 0)


def weight_grads(hid, gg, ug, slots, gslots):
    ff, rows = hid.shape
    depth = slots.shape[1]
    block = 256
    left = pl.BlockSpec((block, rows), lambda i: (i, 0))
    right = pl.BlockSpec((rows, depth), lambda i: (0, 0))
    out = pl.BlockSpec((block, depth), lambda i: (i, 0))
    return pl.pallas_call(
        grads_kernel,
        grid=(ff // block,),
        out_shape=(jax.ShapeDtypeStruct((ff, depth), bf16),) * 3,
        in_specs=[left, left, left, right, right],
        out_specs=[out] * 3,
        compiler_params=pltpu.CompilerParams(vmem_limit_bytes=40000000),
        cost_estimate=pl.CostEstimate(
            flops=6 * ff * rows * depth, bytes_accessed=6 * ff * depth, transcendentals=0
        ),
        name="weight_grads",
    )(hid, gg, ug, slots, gslots)


def per_device(
    tokens, expert_ids, route_share, w_gate, w_up, w_down, reward_head, upstream, pair_order
):
    tok_count, width = tokens.shape
    cap = tok_count * expert_ids.shape[1] // EXPERTS
    seq_total = pair_order.shape[0]
    pack = jnp.concatenate(
        [
            expert_ids.T.astype(f32),
            route_share[None, :],
            jnp.full((5, tok_count), -1.0, f32),
        ],
        axis=0,
    )
    head_rows = jnp.broadcast_to(reward_head[None, :], (8, width))
    pairs = pair_order.reshape(-1, 2)
    slots, gslots, hid, gg, ug, layer_out, grad_tokens, rew, loss = run_layer(
        pack, tokens, upstream, head_rows, pairs, w_gate, w_up, w_down, seq_total, cap
    )
    depth = slots.shape[2]
    grad_down, grad_gate, grad_up = weight_grads(
        hid, gg, ug, slots.reshape(-1, depth), gslots.reshape(-1, depth)
    )
    return (
        layer_out, rew[0, :seq_total], loss[0, 0], grad_tokens, grad_gate, grad_up, grad_down
    )


def solution(mesh):
    in_specs = (
        P("ep", "tp"),
        P("ep", None),
        P("ep"),
        P(("ep", "tp"), None),
        P(("ep", "tp"), None),
        P(("ep", "tp"), None),
        P("tp"),
        P("ep", "tp"),
        P(),
    )
    out_specs = (
        P("ep", "tp"),
        P(),
        P(),
        P("ep", "tp"),
        P(("ep", "tp"), None),
        P(("ep", "tp"), None),
        P(("ep", "tp"), None),
    )
    return jax.shard_map(
        per_device, mesh=mesh, in_specs=in_specs, out_specs=out_specs, check_vma=False
    )
```

time: 180 us -> 117 us (0.65)
  matrix products: 92.6 us -> 0 us
  Pallas kernels: 38.5 us -> 101 us
  between operations: 15.9 us -> 0.66 us
  starting transfers between devices: 11.7 us -> 0 us
  waiting for transfers between devices: 9.82 us -> 0 us
  local copies, waits for them, and re-layouts: 4.14 us -> 12.9 us
  other arithmetic: 6.94 us -> 2 us
    dot_general x14 -> x0, matrix products: 92.6 us -> none  [the longest x1 14.9 us: per_device(): lax.dot_general(slot_rows, w_up, rows_by_cols, preferred_element_type=jnp...]
    pallas_call x2, Pallas kernels: 38.5 us -> 101 us  [the longest x1 80.5 us: run_layer(): pl.pallas_call(partial(layer_kernel, n_ep, n_tp, chunks), out_shape=(shap...]
    all_to_all x2 -> x0, starting transfers between devices: 11.4 us -> none  [return_sums(): lax.all_to_all(partial_sum.reshape(local_width, -1, capacity).astype(jnp....]
    reduce_scatter x2 -> x0, waiting for transfers between devices: 8.07 us -> none  [return_sums(): lax.psum_scatter(sums, 'tp', scatter_dimension=0, tiled=True)]
    unnamed x36 -> x16, local copies, waits for them, and re-layouts: 0.89 us -> 7.85 us
    reduce_sum x12 -> x0, other arithmetic: 2.76 us -> none  [the longest x1 0.94 us: per_device(): jnp.sum(gathered, axis=0).reshape(-1)[:seq_total] / math.sqrt(SEQ_LEN)]
  transfers between devices with their start and end apart: 5 -> 0, of which waited for: 2 -> 0; matrix products, arithmetic and copies ran while one was open for 53% -> 0% of each run, Pallas kernels for 7% -> 0%
where the time goes in v1:
time: 117 us; the launch traced here: 116 us
  Pallas kernels  101 us (86%)
  local copies, waits for them, and re-layouts  12.9 us (11%)
  other arithmetic  2 us (2%)
    pallas_call x1, Pallas kernels, run_layer(): pl.pallas_call(partial(layer_kernel, n_ep, n_tp, chunks), out_shape=(shap...  80.5 us
    pallas_call x1, Pallas kernels, weight_grads(): pl.pallas_call(grads_kernel, grid=(ff // block,), out_shape=(jax.ShapeDty...  20.2 us
    unnamed x16, local copies, waits for them, and re-layouts  7.85 us

profile of v1, /device:TPU:0, one launch (start us, length us, event | category | flops | bytes accessed | tf_op | source)
XLA Modules:
  0.0 116.3 jit_solution(18247518424822002299)
XLA Ops:
  0.6 0.1 pad.2.clone
  0.7 0.7 convert_bitcast_fusion
  1.4 1.3 %maximum_maximum_fusion.pack_ref = f32[8,128]{1,0:T(8,128)} fusion(f32[1,128]{1,0:T(1,128)} %bitcast.10, f32[2,128]{1,0:T(2,128)S(1)} %convert_bitcast_fusion, f32[8]{0:T(128)S(1)} %pad.2.clone), kind=kLoop, calls=%fused_computation | loop fusion | flops 2048 | bytes 5664 | tf_op jit(solution)/shard_map/concatenate | solution.py:632
  2.7 1.3 %reshape.24.pair_ref = s32[8,2]{1,0:T(8,128)} reshape(s32[16]{0:T(128)} %param.17) | data formatting | bytes 128 | tf_op jit(solution)/shard_map/reshape | solution.py:641
  4.0 1.3 %broadcast_in_dim.14.head_ref = f32[8,768]{1,0:T(8,128)} broadcast(f32[768]{0:T(1024)} %param.15), dimensions={1} | broadcast | bytes 27648 | tf_op jit(solution)/shard_map/broadcast_in_dim | solution.py:640
  5.3 80.5 %run_layer.1 = (bf16[8,32,3072]{2,1,0:T(8,128)(2,1)}, bf16[8,32,3072]{2,1,0:T(8,128)(2,1)}, bf16[2048,256]{1,0:T(8,128)(2,1)}, bf16[2048,256]{1,0:T(8,128)(2,1)}...) custom-call(f32[8,128]{1,0:T(8,128)} %maximum_maximum_fusion.pack_re, ...), custom_call_target="tpu_custom_call" | custom-call | tf_op jit(solution)/shard_map/run_layer/pallas_call | solution.py:554
  85.9 1.2 %slice.7 = f32[1,1]{1,0:T(1,128)} slice(f32[8,128]{1,0:T(8,128)} %get-tuple-element.21), slice={[0:1], [0:1]} | slice | bytes 8 | tf_op jit(solution)/shard_map/slice | solution.py:650
  87.1 1.2 %slice_bitcast_fusion = f32[16]{0:T(128)} fusion(f32[8,128]{1,0:T(8,128)} %get-tuple-element.20), kind=kLoop, calls=%fused_computation.2 | loop fusion | bytes 128 | tf_op jit(solution)/shard_map/squeeze | solution.py:650
  88.3 0.0 copy-start
  88.3 1.4 %copy-done = bf16[8,32,3072]{2,1,0:T(8,128)(2,1)S(1)} copy-done((bf16[8,32,3072]{2,1,0:T(8,128)(2,1)S(1)}, bf16[8,32,3072]{2,1,0:T(8,128)(2,1)}, u32[]{:S(2)}) %copy-start) | copy-done | bytes 1572888
  89.7 0.0 copy-start.1
  89.7 1.4 %copy-done.1 = bf16[8,32,3072]{2,1,0:T(8,128)(2,1)S(1)} copy-done((bf16[8,32,3072]{2,1,0:T(8,128)(2,1)S(1)}, bf16[8,32,3072]{2,1,0:T(8,128)(2,1)}, u32[]{:S(2)}) %copy-start.1) | copy-done | bytes 1572888
  91.1 0.0 copy-start.2
  91.1 1.2 %copy-done.2 = bf16[2048,256]{1,0:T(8,128)(2,1)S(1)} copy-done((bf16[2048,256]{1,0:T(8,128)(2,1)S(1)}, bf16[2048,256]{1,0:T(8,128)(2,1)}, u32[]{:S(2)}) %copy-start.2) | copy-done | bytes 1048600
  92.3 0.0 copy-start.3
  92.3 1.2 %copy-done.3 = bf16[2048,256]{1,0:T(8,128)(2,1)S(1)} copy-done((bf16[2048,256]{1,0:T(8,128)(2,1)S(1)}, bf16[2048,256]{1,0:T(8,128)(2,1)}, u32[]{:S(2)}) %copy-start.3) | copy-done | bytes 1048600
  93.5 0.0 copy-start.4
  93.5 1.2 %copy-done.4 = bf16[2048,256]{1,0:T(8,128)(2,1)S(1)} copy-done((bf16[2048,256]{1,0:T(8,128)(2,1)S(1)}, bf16[2048,256]{1,0:T(8,128)(2,1)}, u32[]{:S(2)}) %copy-start.4) | copy-done | bytes 1048600
  94.7 0.0 copy-start.6
  94.8 0.0 copy-start.5
  94.8 20.2 %weight_grads.1 = (bf16[2048,3072]{1,0:T(8,128)(2,1)}, bf16[2048,3072]{1,0:T(8,128)(2,1)}, bf16[2048,3072]{1,0:T(8,128)(2,1)}) custom-call(bf16[2048,256]{1,0:T(8,128)(2,1)S(1)} %copy-done.2, bf16[2048,256]{1,0:T(8,128)(2,1)S(1)} %copy-done.3, bf16[2048,256]{1,0:T(8,128)(2,1)S(1)} %copy-done.4, bf16[256,3072]{1,0:T(8,128)(2,1)S(1)} %bitcast.8, ...), custom_call_target="tpu_custom_call" | custom-call | flops 9663676416 | bytes 37748736 | tf_op jit(solution)/shard_map/weight_grads/pallas_call | solution.py:612
  114.9 0.0 copy-done.6
  114.9 0.7 copy.18
  115.6 0.0 copy-done.5
  115.6 0.7 copy.19
  (1 shorter events, 0.0 us)
Async XLA Ops:
  88.3 1.4 %copy-start = (bf16[8,32,3072]{2,1,0:T(8,128)(2,1)S(1)}, bf16[8,32,3072]{2,1,0:T(8,128)(2,1)}, u32[]{:S(2)}) copy-start(bf16[8,32,3072]{2,1,0:T(8,128)(2,1)} %get-tuple-element.26) | copy-start | bytes 4718596
  89.7 1.4 %copy-start.1 = (bf16[8,32,3072]{2,1,0:T(8,128)(2,1)S(1)}, bf16[8,32,3072]{2,1,0:T(8,128)(2,1)}, u32[]{:S(2)}) copy-start(bf16[8,32,3072]{2,1,0:T(8,128)(2,1)} %get-tuple-element.27) | copy-start | bytes 4718596
  91.1 1.2 %copy-start.2 = (bf16[2048,256]{1,0:T(8,128)(2,1)S(1)}, bf16[2048,256]{1,0:T(8,128)(2,1)}, u32[]{:S(2)}) copy-start(bf16[2048,256]{1,0:T(8,128)(2,1)} %get-tuple-element.23.hid_ref) | copy-start | bytes 3145732
  92.3 1.2 %copy-start.3 = (bf16[2048,256]{1,0:T(8,128)(2,1)S(1)}, bf16[2048,256]{1,0:T(8,128)(2,1)}, u32[]{:S(2)}) copy-start(bf16[2048,256]{1,0:T(8,128)(2,1)} %get-tuple-element.24.gg_ref) | copy-start | bytes 3145732
  93.5 1.2 %copy-start.4 = (bf16[2048,256]{1,0:T(8,128)(2,1)S(1)}, bf16[2048,256]{1,0:T(8,128)(2,1)}, u32[]{:S(2)}) copy-start(bf16[2048,256]{1,0:T(8,128)(2,1)} %get-tuple-element.25.ug_ref) | copy-start | bytes 3145732
  94.7 20.2 %copy-start.6 = (bf16[128,768]{1,0:T(8,128)(2,1)S(1)}, bf16[128,768]{1,0:T(8,128)(2,1)}, u32[]{:S(2)}) copy-start(bf16[128,768]{1,0:T(8,128)(2,1)} %get-tuple-element.38) | copy-start | bytes 589828
  94.8 20.9 %copy-start.5 = (bf16[128,768]{1,0:T(8,128)(2,1)S(1)}, bf16[128,768]{1,0:T(8,128)(2,1)}, u32[]{:S(2)}) copy-start(bf16[128,768]{1,0:T(8,128)(2,1)} %get-tuple-element.41) | copy-start | bytes 589828

commit v2 on v1

v2 whole, which is shorter than its diff:
```python
import math
from functools import partial

import jax
import jax.numpy as jnp
from jax import lax
from jax.experimental import pallas as pl
from jax.experimental.pallas import tpu as pltpu
from jax.sharding import PartitionSpec as P

EXPERTS = 8
SEQ_LEN = 64

loss_scale = 256.0
MESH = pl.DeviceIdType.MESH
NT = (((1,), (1,)), ((), ()))
NN = (((1,), (0,)), ((), ()))
f32 = jnp.float32
bf16 = jnp.bfloat16


def dot(a, b, dims=NN):
    return lax.dot_general(a, b, dims, preferred_element_type=f32)


def remote(src, dst, send_sem, recv_sem, target):
    return pltpu.make_async_remote_copy(
        src_ref=src,
        dst_ref=dst,
        send_sem=send_sem,
        recv_sem=recv_sem,
        device_id=target,
        device_id_type=MESH,
    )


def drain(sent, sem):
    pltpu.make_async_copy(sent, sent, sem).wait()


def layer_kernel(
    n_ep, n_tp, steps, chunks,
    ids_ref, share_ref, tok_hbm, ups_hbm, head_in, pair_ref, wg_ref, wu_ref, wd_ref,
    slots_hbm, gslot_hbm, hid_hbm, gg_hbm, ug_hbm, layer_hbm, gtok_hbm, rew_hbm, loss_hbm,
    slots_ref, gslot_ref, hid_ref, gg_ref, ug_ref, tok_ref, ups_ref, pack_ref, head_ref,
    layer_ref, gtok_ref, rew_ref, loss_ref,
    wgu_v, wd_v, tokb, upsb, raw_all, head_all, hp, hc, mixing, picks, meta, meta_t,
    act_a, act_b, rows_gu, scores, own_row, all_rows, share_row, coef_row, coef_col,
    part_d, pair_d, ybuf_d, sums_d, part_i, pair_i, ybuf_i, sums_i,
    in_sem, out_sem, big_sem, small_sem, w_sem, local_sem, a2a_send, tok_recv, ups_recv, raw_send, raw_recv, head_send, head_recv,
    tok_tp_send, tok_tp_recv, ups_tp_send, ups_tp_recv, rew_send, rew_recv,
    pair_send, pair_recv_d, pair_recv_i, y_send, y_recv_d, y_recv_i, z_send, z_recv_d, z_recv_i,
):
    q = lax.axis_index("ep")
    t = lax.axis_index("tp")
    count = n_ep * n_tp
    me = q * n_tp + t
    n_y = n_tp // 2
    y = t // 2
    core = t % 2
    partner = y * 2 + 1 - core
    tokens, width = tok_ref.shape
    cap = tokb.shape[1]
    replicas = n_ep // EXPERTS
    depth = slots_ref.shape[2]
    rows = n_ep * cap
    ff = wd_v.shape[0]
    fc = ff // chunks
    per = n_ep // chunks
    per_step = n_ep // steps
    fs = ff // steps
    lanes = meta.shape[1]
    seq_local = tokens // SEQ_LEN
    seq_scale = loss_scale / math.sqrt(SEQ_LEN)
    expert = q // replicas

    def chunk(c):
        return pl.ds(pl.multiple_of(c * fc, fc), fc)

    def step_rows(c):
        return pl.ds(pl.multiple_of(c * fs, fs), fs)

    def load(c, i):
        src = (wd_ref, wg_ref, wu_ref)[i]
        at = step_rows(c) if i == 0 else chunk(c)
        dst = wd_v.at[at] if i == 0 else wgu_v.at[c, pl.ds((i - 1) * fc, fc)]
        return pltpu.make_async_copy(src.at[at], dst, w_sem.at[i, c])

    tok_in = pltpu.make_async_copy(tok_hbm, tok_ref, in_sem.at[0])
    ups_in = pltpu.make_async_copy(ups_hbm, ups_ref, in_sem.at[1])
    tok_in.start()
    ups_in.start()

    def keep(i, src, dst, at):
        return pltpu.make_async_copy(src.at[at], dst.at[at], out_sem.at[i])

    barrier = pltpu.get_barrier_semaphore()

    def greet(k, carry):
        other = (me + k) % count
        pl.semaphore_signal(
            barrier, inc=1, device_id=(other // n_tp, other % n_tp), device_id_type=MESH
        )
        return carry

    lax.fori_loop(1, count, greet, 0)

    before = (
        lax.broadcasted_iota(jnp.int32, (tokens, tokens), 0)
        < lax.broadcasted_iota(jnp.int32, (tokens, tokens), 1)
    ).astype(f32).astype(bf16)

    def places(first_id, second_id, wanted):
        first = (first_id == wanted).astype(f32)
        second = (second_id == wanted).astype(f32)
        first_rank = dot(first.astype(bf16), before)
        second_rank = dot(second.astype(bf16), before) + jnp.sum(first, axis=1, keepdims=True)
        return first, first_rank, second, second_rank

    experts_iota = lax.broadcasted_iota(jnp.int32, (EXPERTS, tokens), 0).astype(f32)
    ids = ids_ref[...].astype(f32)
    first_id, second_id, share = ids[0:1], ids[1:2], share_ref[...]
    pack_iota = lax.broadcasted_iota(jnp.int32, pack_ref.shape, 0)
    pack_ref[...] = jnp.where(
        pack_iota == 0, first_id, jnp.where(pack_iota == 1, second_id, share)
    )
    for i in range(width // 128):
        head_ref[:, i * 128 : (i + 1) * 128] = jnp.broadcast_to(head_in[i : i + 1, :], (8, 128))
    first, first_rank, second, second_rank = places(first_id, second_id, experts_iota)

    def slot_of(hot, rank, ids):
        own_rank = jnp.sum(hot * rank, axis=0, keepdims=True)
        return jnp.where(own_rank < cap, ids * cap + own_rank, -1.0)

    first_slot = slot_of(first, first_rank, first_id)
    second_slot = slot_of(second, second_rank, second_id)
    slot_iota = lax.broadcasted_iota(jnp.int32, (EXPERTS * cap, tokens), 0).astype(f32)
    take = ((slot_iota == first_slot) | (slot_iota == second_slot)).astype(f32).astype(bf16)
    tok_in.wait()
    ups_in.wait()
    for i, many in enumerate((steps, chunks, chunks)):
        for c in range(many):
            load(c, i).start()
    tokb[...] = dot(take, tok_ref[...]).astype(bf16).reshape(EXPERTS, cap, width)
    upsb[...] = dot(take, ups_ref[...]).astype(bf16).reshape(EXPERTS, cap, width)
    pl.semaphore_wait(barrier, count - 1)

    def columns(owner):
        return pl.ds(pl.multiple_of(owner * width, 128), width)

    own = q // replicas
    own_tok = pltpu.make_async_copy(tokb.at[own], slots_ref.at[q, :, columns(t)], local_sem.at[0])
    own_ups = pltpu.make_async_copy(upsb.at[own], gslot_ref.at[q, :, columns(t)], local_sem.at[1])
    own_raw = pltpu.make_async_copy(pack_ref, raw_all.at[q], local_sem.at[2])
    own_head = pltpu.make_async_copy(head_ref, head_all.at[t], local_sem.at[3])

    def spread(buf, out, recv, k):
        to = (q + k) % n_ep
        return remote(
            buf.at[to // replicas], out.at[q, :, columns(t)], a2a_send, recv.at[k], (to, t)
        )

    def arrive(buf, out, recv, k):
        source = (q + n_ep - k) % n_ep
        remote(
            buf.at[0], out.at[source, :, columns(t)], a2a_send, recv.at[k], (source, t)
        ).wait_recv()

    for copy in (own_tok, own_head, own_raw, own_ups):
        copy.start()
    for k in range(1, n_tp):
        remote(
            head_ref, head_all.at[t], head_send, head_recv.at[k], (q, (t + k) % n_tp)
        ).start()

    def send_raw(k, carry):
        to = (q + k) % n_ep
        remote(pack_ref, raw_all.at[q], raw_send, raw_recv.at[k], (to, t)).start()
        return carry

    lax.fori_loop(1, n_ep, send_raw, 0)

    def send_tok(k, carry):
        spread(tokb, slots_ref, tok_recv, k).start()
        return carry

    lax.fori_loop(1, n_ep, send_tok, 0)

    def hand_on(out, sems, k, owner, target, row):
        send, recv = sems
        piece = out.at[(q + n_ep - k) % n_ep, :, columns(owner)]
        return remote(piece, piece, send, recv.at[row, k], (q, target))

    def pass_on(out, sems, k):
        for j in range(1, n_y):
            hand_on(out, sems, k, t, (t + 2 * j) % n_tp, j - 1).start()
        hand_on(out, sems, k, t, partner, n_y - 1).start()

    def forward(out, sems, k):
        for j in range(1, n_y):
            origin = (t + n_tp - 2 * j) % n_tp
            hand_on(out, sems, k, origin, t, j - 1).wait_recv()
            hand_on(out, sems, k, origin, partner, n_y - 1 + j).start()

    def finish(out, sems):
        def one(k, carry):
            hand_on(out, sems, k, partner, t, n_y - 1).wait_recv()
            for j in range(1, n_y):
                origin = (partner + n_tp - 2 * j) % n_tp
                hand_on(out, sems, k, origin, t, n_y - 1 + j).wait_recv()
            return carry

        lax.fori_loop(0, n_ep, one, 0)

    lag = min(2, n_ep)
    tok_sems = (tok_tp_send, tok_tp_recv)
    ups_sems = (ups_tp_send, ups_tp_recv)

    def step_piece(buf, out, recv, sems, k):
        arrive(buf, out, recv, k)
        pass_on(out, sems, k)

        @pl.when(k >= lag)
        def _():
            forward(out, sems, k - lag)

    def last_pieces(out, sems):
        for k in range(n_ep - lag, n_ep):
            forward(out, sems, k)

    own_tok.wait()
    pass_on(slots_ref, tok_sems, 0)

    own_head.wait()
    tok_f = tok_ref[...].astype(f32)
    head_mine = head_ref[0:1, :]
    own_scores = jnp.sum(tok_f * head_mine, axis=1, keepdims=True)
    token_iota = lax.broadcasted_iota(jnp.int32, (tokens, lanes), 0)
    lane_iota = lax.broadcasted_iota(jnp.int32, (tokens, lanes), 1)
    token_seq = token_iota // SEQ_LEN + q * seq_local
    in_seq = token_seq == lane_iota
    own_row[...] = jnp.broadcast_to(
        jnp.sum(jnp.where(in_seq, own_scores, 0.0), axis=0, keepdims=True), own_row.shape
    )

    back_iota = lax.broadcasted_iota(jnp.int32, (rows, tokens), 0)
    back_slot = ((back_iota // (replicas * cap)) * cap + back_iota % cap).astype(f32)
    is_first = back_slot == first_slot
    is_second = back_slot == second_slot
    mix_t = jnp.where(is_first, share, 0.0) + jnp.where(is_second, 1.0 - share, 0.0)
    mixing[...] = mix_t.T
    picks[...] = (is_first | is_second).astype(f32).T.astype(bf16)

    for k in range(1, n_tp):
        source = (t + n_tp - k) % n_tp
        remote(head_ref, head_all.at[source], head_send, head_recv.at[k], (q, source)).wait_recv()
    part_iota = lax.broadcasted_iota(jnp.int32, (hp.shape[0], width), 0)
    for owner in range(n_tp):
        rest = head_all[owner][0:1, :]
        stacked = jnp.zeros((hp.shape[0], width), f32)
        for i in range(3):
            piece = rest.astype(bf16).astype(f32)
            stacked = jnp.where(part_iota == i, piece, stacked)
            rest = rest - piece
        hp[:, owner * width : (owner + 1) * width] = stacked.astype(bf16)

    cap_iota = lax.broadcasted_iota(jnp.int32, (cap, tokens), 0).astype(f32)
    cap_token = lax.broadcasted_iota(jnp.int32, (cap, tokens), 1) // SEQ_LEN
    cap_lane = lax.broadcasted_iota(jnp.int32, (cap, lanes), 1)
    expert_f = expert.astype(f32)

    def block_meta(b):
        raw = raw_all[b]
        hot = (raw == expert_f).astype(f32)
        rank = dot(hot.astype(bf16), before)
        first_hot, second_hot = hot[0:1], hot[1:2]
        second_of = rank[1:2] + jnp.sum(first_hot, axis=1, keepdims=True)
        first_at = jnp.where((first_hot > 0.0) & (rank[0:1] < cap), rank[0:1], -1.0)
        second_at = jnp.where((second_hot > 0.0) & (second_of < cap), second_of, -1.0)
        share_b = raw[2:3]
        shares = jnp.where(cap_iota == first_at, share_b, 0.0) + jnp.where(
            cap_iota == second_at, 1.0 - share_b, 0.0
        )
        spreaded = jnp.zeros((cap, lanes), f32)
        for s in range(seq_local):
            column = jnp.sum(jnp.where(cap_token == s, shares, 0.0), axis=1, keepdims=True)
            spreaded = jnp.where(cap_lane == b * seq_local + s, column, spreaded)
        meta[pl.ds(pl.multiple_of(b * cap, cap), cap), :] = spreaded

    def token_phase(c, carry):
        for j in range(per_step):
            k = c * per_step + j
            source = (q + n_ep - k) % n_ep

            @pl.when(k > 0)
            def _():
                step_piece(tokb, slots_ref, tok_recv, tok_sems, k)
                spread(upsb, gslot_ref, ups_recv, k).start()
                remote(
                    pack_ref, raw_all.at[source], raw_send, raw_recv.at[k], (source, t)
                ).wait_recv()

            block_meta(source)

        load(c, 0).wait()
        head_dot = dot(wd_v[step_rows(c), :], hp[...], NT)
        hc[step_rows(c), :] = jnp.broadcast_to(
            jnp.sum(head_dot, axis=1, keepdims=True), (fs, 128)
        )
        return carry

    own_raw.wait()
    lax.fori_loop(0, steps, token_phase, 0)
    last_pieces(slots_ref, tok_sems)
    meta_t[...] = meta[...].T
    share_row[...] = jnp.broadcast_to(
        jnp.sum(meta_t[...], axis=0, keepdims=True), share_row.shape
    )
    finish(slots_ref, tok_sems)
    slots_out = pltpu.make_async_copy(slots_ref, slots_hbm, big_sem.at[0])
    slots_out.start()

    scores[...] = jnp.zeros_like(scores)

    def gate_up(c):
        load(c, 1).wait()
        load(c, 2).wait()
        slot_rows = slots_ref[...].reshape(rows, depth)
        return dot(wgu_v[c], slot_rows, NT)

    def wide(column):
        return jnp.concatenate([column] * (rows // 128), axis=1)

    def activate(c, products):
        gate, up = products[:fc], products[fc:]
        sigmoid = jax.nn.sigmoid(gate)
        silu = gate * sigmoid
        act_b[chunk(c), :] = silu
        act_a[chunk(c), :] = up * (sigmoid * (1.0 + gate * (1.0 - sigmoid)))
        hidden = (silu * up).astype(bf16)
        hid_ref[chunk(c), :] = hidden
        hidden_f = hidden.astype(f32)
        rows_gu[:, chunk(c)] = hidden_f.T.astype(bf16)
        scores[...] += jnp.sum(
            hidden_f * wide(hc[chunk(c), :]), axis=0, keepdims=True
        )

    def pass_ups(c):
        for j in range(per):
            k = c * per + j

            @pl.when(k > 0)
            def _():
                step_piece(upsb, gslot_ref, ups_recv, ups_sems, k)

    def forward_phase(c, carry):
        pass_ups(c - 1)
        following = gate_up(c)
        activate(c - 1, carry)
        keep(0, hid_ref, hid_hbm, chunk(c - 1)).start()
        return following

    own_ups.wait()
    pass_on(gslot_ref, ups_sems, 0)
    last = lax.fori_loop(1, chunks, forward_phase, gate_up(0))
    activate(chunks - 1, last)
    keep(0, hid_ref, hid_hbm, chunk(chunks - 1)).start()

    by_seq = jnp.sum(meta_t[...] * scores[0:1, :], axis=1, keepdims=True)
    mine = own_row[...] + jnp.broadcast_to(by_seq, (lanes, lanes)).T[0:8]
    all_rows[me] = mine

    def send_row(k, carry):
        other = (me + k) % count
        remote(
            all_rows.at[me], all_rows.at[me], rew_send, rew_recv, (other // n_tp, other % n_tp)
        ).start()
        return carry

    lax.fori_loop(1, count, send_row, 0)

    pass_ups(chunks - 1)

    def within(span):
        return pl.ds(*span)

    def product(part, target, left, weight, span):
        first, size = span
        cols = pl.ds(pl.multiple_of(target * width + first, 128), size)
        total = dot(left[...], weight[:, cols])
        part[target, :, :, within(span)] = total.astype(bf16).reshape(n_ep, cap, size)

    def to_pair(part, pair, recv, span, yy):
        return remote(
            part.at[yy * 2 + 1 - core, :, :, within(span)], pair.at[yy, :, :, within(span)],
            pair_send, recv.at[yy], (q, partner),
        )

    def from_pair(part, pair, recv, span, yy):
        remote(
            part.at[yy * 2 + core, :, :, within(span)], pair.at[yy, :, :, within(span)],
            pair_send, recv.at[yy], (q, partner),
        ).wait_recv()

    def over_y(part, pair, ybuf, recv, span, r, k):
        yy = (y + r) % n_y
        blk = (q + k) % n_ep
        mine_at = (yy * 2 + core, blk, slice(None), within(span))
        here = part[mine_at].astype(f32) + pair[yy, blk, :, within(span)].astype(f32)
        part[mine_at] = here.astype(bf16)
        remote(
            part.at[mine_at], ybuf.at[y, blk, :, within(span)], y_send, recv.at[r - 1, k],
            (q, yy * 2 + core),
        ).start()

    def over_z(part, pair, ybuf, sums, y_recv, z_recv, span, k):
        blk = (q + k) % n_ep
        mine_at = (t, blk, slice(None), within(span))
        total = part[mine_at].astype(f32) + pair[y, blk, :, within(span)].astype(f32)
        for r in range(1, n_y):
            source = (y + n_y - r) % n_y
            remote(
                part.at[mine_at], ybuf.at[source, blk, :, within(span)], y_send,
                y_recv.at[r - 1, k], (q, source * 2 + core),
            ).wait_recv()
            total = total + ybuf[source, blk, :, within(span)].astype(f32)

        @pl.when(k == 0)
        def _():
            sums[q, :, within(span)] = total.astype(bf16)

        @pl.when(k > 0)
        def _():
            part[mine_at] = total.astype(bf16)
            remote(
                part.at[mine_at], sums.at[q, :, within(span)], z_send, z_recv.at[k], (blk, t)
            ).start()

    def all_back(part, sums, z_recv, span):
        def one(k, carry):
            source = (q + n_ep - k) % n_ep
            remote(
                part.at[t, 0, :, within(span)], sums.at[source, :, within(span)], z_send,
                z_recv.at[k], (source, t),
            ).wait_recv()
            return carry

        lax.fori_loop(1, n_ep, one, 0)

    full = (0, width)
    cut = width // 128 * 2 // 3 * 128
    spans = ((0, cut), (cut, width - cut))
    rows_h = rows_gu.at[:, pl.ds(0, ff)]

    def down_phase(j, carry):
        yy = (y + 1 + j) % n_y
        product(part_d, yy * 2 + 1 - core, rows_h, wd_v, full)
        to_pair(part_d, pair_d, pair_recv_d, full, yy).start()
        product(part_d, yy * 2 + core, rows_h, wd_v, full)
        return carry

    lax.fori_loop(0, n_y, down_phase, 0)
    last_pieces(gslot_ref, ups_sems)
    for r in range(n_y):
        from_pair(part_d, pair_d, pair_recv_d, full, (y + r) % n_y)
    finish(gslot_ref, ups_sems)

    rest_rows = all_rows.at[pl.ds(0, count - 1)]
    pltpu.make_async_copy(rest_rows, rest_rows, rew_recv).wait()
    rewards = jnp.sum(all_rows[...], axis=0)[0:1] / math.sqrt(SEQ_LEN)
    seq_total = pair_ref.shape[1]
    rew_ref[...] = rewards[:, :seq_total]
    pairs = seq_total // 2
    pair_lane = lax.broadcasted_iota(jnp.int32, (pairs, lanes), 1).astype(f32)
    order_lane = lax.broadcasted_iota(jnp.int32, (pairs, seq_total), 1)
    order_pair = 2 * lax.broadcasted_iota(jnp.int32, (pairs, seq_total), 0)
    order = pair_ref[...].astype(f32)

    def members(which):
        taken = jnp.where(order_lane == order_pair + which, order, 0.0)
        return (pair_lane == jnp.sum(taken, axis=1, keepdims=True)).astype(f32)

    chosen, rejected = members(0), members(1)
    margin = jnp.sum((chosen - rejected) * rewards, axis=1, keepdims=True)
    losses = jnp.maximum(-margin, 0.0) + jnp.log1p(jnp.exp(-jnp.abs(margin)))
    loss_ref[...] = jnp.sum(losses, axis=0, keepdims=True) / pairs
    pair_weight = jax.nn.sigmoid(-margin)
    seq_coef = jnp.sum(pair_weight * (rejected - chosen), axis=0, keepdims=True)
    slot_coef = seq_scale * jnp.sum(
        jnp.where(meta[...] > 0.0, seq_coef, 0.0), axis=1, keepdims=True
    )
    coef_wide = jnp.broadcast_to(slot_coef, coef_col.shape)
    coef_col[...] = coef_wide
    coef_row[...] = coef_wide.T[0:8]

    pieces = 1
    groups = chunks // pieces
    gc = fc * pieces

    def group(c):
        return pl.ds(pl.multiple_of(c * gc, gc), gc)

    def sums_over_y(c):
        for j in range(per * pieces):
            for r in range(1, n_y):
                over_y(part_d, pair_d, ybuf_d, y_recv_d, full, r, c * per * pieces + j)

    def upstream(c):
        return dot(wd_v[group(c), :], gslot_ref[...].reshape(rows, depth), NT)

    def gradients(c, columns_up):
        hidden_grad = share_row[0:1, :] * (
            columns_up + coef_row[0:1, :] * wide(hc[group(c), :])
        )
        gate_grad = (hidden_grad * act_a[group(c), :]).astype(bf16)
        up_grad = (hidden_grad * act_b[group(c), :]).astype(bf16)
        gg_ref[group(c), :] = gate_grad
        ug_ref[group(c), :] = up_grad
        keep(1, gg_ref, gg_hbm, group(c)).start()
        keep(2, ug_ref, ug_hbm, group(c)).start()
        gate_t = gate_grad.astype(f32).T.astype(bf16)
        up_t = up_grad.astype(f32).T.astype(bf16)
        for i in range(pieces):
            first_at = (c * pieces + i) * 2 * fc
            part_of = slice(i * fc, (i + 1) * fc)
            rows_gu[:, pl.ds(pl.multiple_of(first_at, fc), fc)] = gate_t[:, part_of]
            rows_gu[:, pl.ds(pl.multiple_of(first_at + fc, fc), fc)] = up_t[:, part_of]

    def gradient_phase(c, carry):
        sums_over_y(c)
        following = upstream(c)
        gradients(c - 1, carry)
        return following

    sums_over_y(0)
    last_up = lax.fori_loop(1, groups, gradient_phase, upstream(0))
    gradients(groups - 1, last_up)

    both = wgu_v.reshape(2 * ff, depth)

    share_of = n_ep // n_tp

    def back_some(i):
        for j in range(share_of):
            k = i * share_of + j
            over_z(part_d, pair_d, ybuf_d, sums_d, y_recv_d, z_recv_d, full, (k + 1) % n_ep)

    def return_some(h, i):
        for j in range(share_of):
            k = i * share_of + j
            over_z(
                part_i, pair_i, ybuf_i, sums_i, y_recv_i.at[h], z_recv_i.at[h], spans[h],
                (k + 1) % n_ep,
            )

    def serve(h, i):
        if h == 0:
            back_some(i)
        else:
            return_some(0, i)

    for h in range(2):
        def input_phase(j, carry, h=h):
            yy = (y + 1 + j) % n_y
            product(part_i, yy * 2 + 1 - core, rows_gu, both, spans[h])
            to_pair(part_i, pair_i, pair_recv_i.at[h], spans[h], yy).start()
            serve(h, 2 * j)
            product(part_i, yy * 2 + core, rows_gu, both, spans[h])
            serve(h, 2 * j + 1)
            from_pair(part_i, pair_i, pair_recv_i.at[h], spans[h], yy)

            @pl.when(j < n_y - 1)
            def _():
                def one(k, carry_k):
                    over_y(part_i, pair_i, ybuf_i, y_recv_i.at[h], spans[h], j + 1, k)
                    return carry_k

                lax.fori_loop(0, n_ep, one, 0)

            return carry

        lax.fori_loop(0, n_y, input_phase, 0)

    drain(gslot_ref.at[:, :, pl.ds(0, (n_tp - 1) * width)], ups_tp_send)

    def tail_phase(k, carry):
        row_at = pl.ds(pl.multiple_of(k * cap, cap), cap)
        coef_k = coef_col[row_at, 0:1]
        share_k = jnp.sum(meta[row_at, :], axis=1, keepdims=True)
        for owner in range(n_tp):
            cols = pl.ds(owner * width, width)
            head_k = head_all[owner][0:1, :]
            slot_out = (gslot_ref[k, :, cols].astype(f32) + coef_k * head_k).astype(bf16)
            gslot_ref[k, :, cols] = (share_k * slot_out.astype(f32)).astype(bf16)
        over_z(
            part_i, pair_i, ybuf_i, sums_i, y_recv_i.at[1], z_recv_i.at[1], spans[1],
            (k + 1) % n_ep,
        )
        pltpu.make_async_copy(gslot_ref.at[k], gslot_hbm.at[k], big_sem.at[1]).start()
        return carry

    lax.fori_loop(0, n_ep, tail_phase, 0)

    all_back(part_d, sums_d, z_recv_d, full)
    rest = mixing[...]
    mixed = tok_ref[...].astype(f32)
    expert_sums = sums_d[...].reshape(rows, width)
    for _ in range(3):
        piece = rest.astype(bf16)
        mixed = mixed + dot(piece, expert_sums)
        rest = rest - piece.astype(f32)
    layer_ref[...] = mixed.astype(bf16)
    finals = [
        pltpu.make_async_copy(src, dst, small_sem.at[i])
        for i, (src, dst) in enumerate(
            (
                (layer_ref, layer_hbm), (rew_ref, rew_hbm),
                (loss_ref, loss_hbm), (gtok_ref, gtok_hbm),
            )
        )
    ]
    for copy in finals[:3]:
        copy.start()
    token_coef = jnp.sum(jnp.where(in_seq, seq_coef, 0.0), axis=1, keepdims=True)
    grad_out = (ups_ref[...].astype(f32) + seq_scale * token_coef * head_mine).astype(bf16)
    for h in range(2):
        all_back(part_i, sums_i, z_recv_i.at[h], spans[h])
    returned = dot(picks[...], sums_i[...].reshape(rows, width))
    gtok_ref[...] = (grad_out.astype(f32) + returned).astype(bf16)
    finals[3].start()

    for copy in finals:
        copy.wait()
    slots_out.wait()
    pltpu.make_async_copy(gslot_ref, gslot_hbm, big_sem.at[1]).wait()
    for i, (src, dst) in enumerate(((hid_ref, hid_hbm), (gg_ref, gg_hbm), (ug_ref, ug_hbm))):
        keep(i, src, dst, pl.ds(0, ff)).wait()
    drain(sums_d.at[pl.ds(0, n_ep - 1)], a2a_send)
    drain(sums_d.at[pl.ds(0, n_ep - 1)], a2a_send)
    drain(raw_all.at[pl.ds(0, n_ep - 1)], raw_send)
    drain(head_all.at[pl.ds(0, n_tp - 1)], head_send)
    drain(slots_ref.at[:, :, pl.ds(0, (n_tp - 1) * width)], tok_tp_send)
    drain(rest_rows, rew_send)
    for _ in range(2):
        drain(pair_d, pair_send)
        if n_y > 1:
            drain(ybuf_d.at[pl.ds(0, n_y - 1)], y_send)
        drain(sums_d.at[pl.ds(0, n_ep - 1)], z_send)


def run_layer(
    expert_ids, share, tokens, upstream, head, order, w_gate, w_up, w_down, cap
):
    n_ep = lax.axis_size("ep")
    n_tp = lax.axis_size("tp")
    n_y = n_tp // 2
    tok_count, width = tokens.shape
    ff, depth = w_gate.shape
    rows = n_ep * cap
    steps = math.gcd(ff // 256, n_ep)
    chunks = max(steps // 2, 1)
    fc = ff // chunks
    seq_total = order.shape[1]
    lanes = 128 * pl.cdiv(seq_total, 128)
    dma = pltpu.SemaphoreType.DMA
    vmem = pl.BlockSpec(memory_space=pltpu.VMEM)
    hbm = pl.BlockSpec(memory_space=pl.ANY)

    def shape(*dims, kind=bf16):
        return jax.ShapeDtypeStruct(dims, kind)

    def scratch(*dims, kind=bf16):
        return pltpu.VMEM(dims, kind)

    back = [
        scratch(n_tp, n_ep, cap, width), scratch(n_y, n_ep, cap, width),
        scratch(n_y, n_ep, cap, width), scratch(n_ep, cap, width),
    ]
    return pl.pallas_call(
        partial(layer_kernel, n_ep, n_tp, steps, chunks),
        out_shape=(
            shape(n_ep, cap, depth), shape(n_ep, cap, depth),
            shape(ff, rows), shape(ff, rows), shape(ff, rows),
            shape(tok_count, width), shape(tok_count, width),
            shape(1, seq_total, kind=f32), shape(1, 1, kind=f32),
        ),
        in_specs=[vmem] * 2 + [hbm] * 2 + [vmem] * 2 + [hbm] * 3,
        out_specs=[hbm] * 9,
        scratch_shapes=[
            scratch(n_ep, cap, depth), scratch(n_ep, cap, depth),
            scratch(ff, rows), scratch(ff, rows), scratch(ff, rows),
            scratch(tok_count, width), scratch(tok_count, width),
            scratch(8, tok_count, kind=f32), scratch(8, width, kind=f32),
            scratch(tok_count, width), scratch(tok_count, width),
            scratch(1, seq_total, kind=f32), scratch(1, 1, kind=f32),
            scratch(chunks, 2 * fc, depth), scratch(ff, depth),
            scratch(EXPERTS, cap, width), scratch(EXPERTS, cap, width),
            scratch(n_ep, 8, tok_count, kind=f32), scratch(n_tp, 8, width, kind=f32),
            scratch(16, depth), scratch(ff, 128, kind=f32),
            scratch(tok_count, rows, kind=f32), scratch(tok_count, rows),
            scratch(rows, lanes, kind=f32), scratch(lanes, rows, kind=f32),
            scratch(ff, rows, kind=f32), scratch(ff, rows, kind=f32),
            scratch(rows, 2 * ff),
            scratch(8, rows, kind=f32), scratch(8, lanes, kind=f32),
            scratch(n_ep * n_tp, 8, lanes, kind=f32),
            scratch(8, rows, kind=f32), scratch(8, rows, kind=f32), scratch(rows, 128, kind=f32),
        ] + back + back + [
            dma((2,)), dma((3,)), dma((2,)), dma((4,)),
            dma((3, steps)), dma((4,)), dma, dma((n_ep,)), dma((n_ep,)), dma, dma((n_ep,)),
            dma, dma((n_tp,)), dma, dma((n_tp - 1, n_ep)), dma, dma((n_tp - 1, n_ep)), dma, dma,
            dma, dma((n_y,)), dma((2, n_y)), dma, dma((n_y - 1, n_ep)), dma((2, n_y - 1, n_ep)),
            dma, dma((n_ep,)), dma((2, n_ep)),
        ],
        compiler_params=pltpu.CompilerParams(
            collective_id=0, has_side_effects=True, vmem_limit_bytes=67000000
        ),
        name="run_layer",
    )(expert_ids, share, tokens, upstream, head, order, w_gate, w_up, w_down)


def grads_kernel(
    hid_ref, gg_ref, ug_ref, slots_ref, gslot_ref, layer_in, gtok_in, rew_in, loss_in,
    down_ref, gate_ref, up_ref, layer_ref, gtok_ref, rew_ref, loss_ref,
):
    @pl.when(pl.program_id(0) == 0)
    def _():
        layer_ref[...] = layer_in[...]
        gtok_ref[...] = gtok_in[...]
        rew_ref[...] = rew_in[...]
        loss_ref[...] = loss_in[...]

    inputs = slots_ref[...]
    down_ref[...] = dot(hid_ref[...], gslot_ref[...]).astype(bf16)
    gate_ref[...] = dot(gg_ref[...], inputs).astype(bf16)
    up_ref[...] = dot(ug_ref[...], inputs).astype(bf16)


def weight_grads(hid, gg, ug, slots, gslots, *small):
    ff, rows = hid.shape
    depth = slots.shape[1]
    block = 512 if depth % 512 == 0 else 128

    def whole(array):
        return pl.BlockSpec(array.shape, lambda i: (0, 0))

    left = pl.BlockSpec((ff, rows), lambda i: (0, 0))
    right = pl.BlockSpec((rows, block), lambda i: (0, i))
    out = pl.BlockSpec((ff, block), lambda i: (0, i))
    return pl.pallas_call(
        grads_kernel,
        grid=(depth // block,),
        out_shape=(jax.ShapeDtypeStruct((ff, depth), bf16),) * 3
        + tuple(jax.ShapeDtypeStruct(array.shape, array.dtype) for array in small),
        in_specs=[left, left, left, right, right] + [whole(array) for array in small],
        out_specs=[out] * 3 + [whole(array) for array in small],
        compiler_params=pltpu.CompilerParams(vmem_limit_bytes=67000000),
        cost_estimate=pl.CostEstimate(
            flops=6 * ff * rows * depth, bytes_accessed=6 * ff * depth, transcendentals=0
        ),
        name="weight_grads",
    )(hid, gg, ug, slots, gslots, *small)


def per_device(
    tokens, expert_ids, route_share, w_gate, w_up, w_down, reward_head, upstream, pair_order
):
    tok_count = tokens.shape[0]
    cap = tok_count * expert_ids.shape[1] // EXPERTS
    slots, gslots, hid, gg, ug, *small = run_layer(
        expert_ids.T, route_share.reshape(1, -1), tokens, upstream, reward_head.reshape(-1, 128),
        pair_order.reshape(1, -1), w_gate, w_up, w_down, cap,
    )
    depth = slots.shape[2]
    grad_down, grad_gate, grad_up, layer_out, grad_tokens, rew, loss = weight_grads(
        hid, gg, ug, slots.reshape(-1, depth), gslots.reshape(-1, depth), *small
    )
    return (
        layer_out, rew.reshape(-1), loss.reshape(()), grad_tokens, grad_gate, grad_up, grad_down
    )


def solution(mesh):
    in_specs = (
        P("ep", "tp"),
        P("ep", None),
        P("ep"),
        P(("ep", "tp"), None),
        P(("ep", "tp"), None),
        P(("ep", "tp"), None),
        P("tp"),
        P("ep", "tp"),
        P(),
    )
    out_specs = (
        P("ep", "tp"),
        P(),
        P(),
        P("ep", "tp"),
        P(("ep", "tp"), None),
        P(("ep", "tp"), None),
        P(("ep", "tp"), None),
    )
    return jax.shard_map(
        per_device, mesh=mesh, in_specs=in_specs, out_specs=out_specs, check_vma=False
    )
```

time: 117 us -> 89.5 us (0.76)
  local copies, waits for them, and re-layouts: 12.9 us -> 0 us
  Pallas kernels: 101 us -> 88.6 us
  other arithmetic: 2 us -> 0 us
    pallas_call x2, Pallas kernels: 101 us -> 88.6 us  [the longest x1 72 us: run_layer(): pl.pallas_call(partial(layer_kernel, n_ep, n_tp, steps, chunks), out_shap...]
    unnamed x16 -> x0, local copies, waits for them, and re-layouts: 7.85 us -> none
    reshape x1 -> x0, local copies, waits for them, and re-layouts: 1.33 us -> none  [per_device(): pairs = pair_order.reshape(-1, 2)]
    concatenate x1 -> x0, other arithmetic: 1.32 us -> none  [per_device(): jnp.concatenate([expert_ids.T.astype(f32), route_share[None, :], jnp.full...]
    broadcast_in_dim x2 -> x0, local copies, waits for them, and re-layouts: 1.3 us -> none  [the longest x1 1.3 us: per_device(): head_rows = jnp.broadcast_to(reward_head[None, :], (8, width))]
    slice x1 -> x0, local copies, waits for them, and re-layouts: 1.19 us -> none  [per_device(): loss[0, 0]]
    squeeze x1 -> x0, local copies, waits for them, and re-layouts: 1.18 us -> none  [per_device(): rew[0, :seq_total]]
where the time goes in v2:
time: 89.5 us; the launch traced here: 89.3 us
  Pallas kernels  88.6 us (99%)
    pallas_call x1, Pallas kernels, run_layer(): pl.pallas_call(partial(layer_kernel, n_ep, n_tp, steps, chunks), out_shap...  72 us
    pallas_call x1, Pallas kernels, weight_grads(): pl.pallas_call(grads_kernel, grid=(depth // block,), out_shape=(jax.Shape...  16.6 us

profile of v2, /device:TPU:0, one launch (start us, length us, event | category | flops | bytes accessed | tf_op | source)
XLA Modules:
  0.0 89.3 jit_solution(8444448025093522853)
XLA Ops:
  0.6 72.0 %run_layer.1 = (bf16[8,32,3072]{2,1,0:T(8,128)(2,1)}, bf16[8,32,3072]{2,1,0:T(8,128)(2,1)}, bf16[2048,256]{1,0:T(8,128)(2,1)}, bf16[2048,256]{1,0:T(8,128)(2,1)}...) custom-call(s32[2,128]{1,0:T(2,128)} %bitcast.9, ...), custom_call_target="tpu_custom_call" | custom-call | tf_op jit(solution)/shard_map/run_layer/pallas_call | solution.py:679
  72.7 16.6 %weight_grads.1 = (bf16[2048,3072]{1,0:T(8,128)(2,1)}, bf16[2048,3072]{1,0:T(8,128)(2,1)}, bf16[2048,3072]{1,0:T(8,128)(2,1)}, bf16[128,768]{1,0:T(8,128)(2,1)},...) custom-call(bf16[2048,256]{1,0:T(8,128)(2,1)} %get-tuple-element.23.hid_ref, ...), custom_call_target="tpu_custom_call" | custom-call | flops 9663676416 | bytes 37748736 | tf_op jit(solution)/shard_map/weight_grads/pallas_call | solution.py:749

commit v3 on v2

--- a/solution.py
+++ b/solution.py
@@ -457,12 +457,20 @@
         product(part_d, yy * 2 + 1 - core, rows_h, wd_v, full)
         to_pair(part_d, pair_d, pair_recv_d, full, yy).start()
         product(part_d, yy * 2 + core, rows_h, wd_v, full)
+        from_pair(part_d, pair_d, pair_recv_d, full, yy)
+
+        @pl.when(j < n_y - 1)
+        def _():
+            def one(k, carry_k):
+                over_y(part_d, pair_d, ybuf_d, y_recv_d, full, j + 1, k)
+                return carry_k
+
+            lax.fori_loop(0, n_ep, one, 0)
+
         return carry
 
     lax.fori_loop(0, n_y, down_phase, 0)
     last_pieces(gslot_ref, ups_sems)
-    for r in range(n_y):
-        from_pair(part_d, pair_d, pair_recv_d, full, (y + r) % n_y)
     finish(gslot_ref, ups_sems)
 
     rest_rows = all_rows.at[pl.ds(0, count - 1)]
@@ -500,10 +508,10 @@
     def group(c):
         return pl.ds(pl.multiple_of(c * gc, gc), gc)
 
-    def sums_over_y(c):
-        for j in range(per * pieces):
-            for r in range(1, n_y):
-                over_y(part_d, pair_d, ybuf_d, y_recv_d, full, r, c * per * pieces + j)
+    def back_some(c):
+        for j in range(per):
+            k = c * per + j
+            over_z(part_d, pair_d, ybuf_d, sums_d, y_recv_d, z_recv_d, full, (k + 1) % n_ep)
 
     def upstream(c):
         return dot(wd_v[group(c), :], gslot_ref[...].reshape(rows, depth), NT)
@@ -527,23 +535,18 @@
             rows_gu[:, pl.ds(pl.multiple_of(first_at + fc, fc), fc)] = up_t[:, part_of]
 
     def gradient_phase(c, carry):
-        sums_over_y(c)
+        back_some(c - 1)
         following = upstream(c)
         gradients(c - 1, carry)
         return following
 
-    sums_over_y(0)
     last_up = lax.fori_loop(1, groups, gradient_phase, upstream(0))
+    back_some(groups - 1)
     gradients(groups - 1, last_up)
 
     both = wgu_v.reshape(2 * ff, depth)
 
     share_of = n_ep // n_tp
-
-    def back_some(i):
-        for j in range(share_of):
-            k = i * share_of + j
-            over_z(part_d, pair_d, ybuf_d, sums_d, y_recv_d, z_recv_d, full, (k + 1) % n_ep)
 
     def return_some(h, i):
         for j in range(share_of):
@@ -554,9 +557,7 @@
             )
 
     def serve(h, i):
-        if h == 0:
-            back_some(i)
-        else:
+        if h == 1:
             return_some(0, i)
 
     for h in range(2):

time: 89.5 us -> 88.6 us (0.990)
  no operation moved by 1% of the time
where the time goes in v3:
time: 88.6 us; the launch traced here: 88.4 us
  Pallas kernels  87.8 us (99%)
    pallas_call x1, Pallas kernels, run_layer(): pl.pallas_call(partial(layer_kernel, n_ep, n_tp, steps, chunks), out_shap...  71.2 us
    pallas_call x1, Pallas kernels, weight_grads(): pl.pallas_call(grads_kernel, grid=(depth // block,), out_shape=(jax.Shape...  16.6 us

profile of v3, /device:TPU:0, one launch (start us, length us, event | category | flops | bytes accessed | tf_op | source)
XLA Modules:
  0.0 88.4 jit_solution(16918431406017390026)
XLA Ops:
  0.6 71.2 %run_layer.1 = (bf16[8,32,3072]{2,1,0:T(8,128)(2,1)}, bf16[8,32,3072]{2,1,0:T(8,128)(2,1)}, bf16[2048,256]{1,0:T(8,128)(2,1)}, bf16[2048,256]{1,0:T(8,128)(2,1)}...) custom-call(s32[2,128]{1,0:T(2,128)} %bitcast.9, ...), custom_call_target="tpu_custom_call" | custom-call | tf_op jit(solution)/shard_map/run_layer/pallas_call | solution.py:680
  71.8 16.6 %weight_grads.1 = (bf16[2048,3072]{1,0:T(8,128)(2,1)}, bf16[2048,3072]{1,0:T(8,128)(2,1)}, bf16[2048,3072]{1,0:T(8,128)(2,1)}, bf16[128,768]{1,0:T(8,128)(2,1)},...) custom-call(bf16[2048,256]{1,0:T(8,128)(2,1)} %get-tuple-element.23.hid_ref, ...), custom_call_target="tpu_custom_call" | custom-call | flops 9663676416 | bytes 37748736 | tf_op jit(solution)/shard_map/weight_grads/pallas_call | solution.py:750
